TPU v7x, 32 devices: a whole 2x2x4 slice. The times are simulated.
32 devices in a mesh: cp: 8 (over y, x, core), tp: 4 (over z).
Axes of the slice: x: 2, y: 2, z: 4, core: 2. Of those that a mesh axis runs over, the one named last changes fastest.
Arguments:
- hidden: bfloat16 [2048, 4096], P('cp', 'tp'), may hold values from -120 to 120
- query_weight: bfloat16 [4096, 4096], P(None, 'tp'), may hold values from -0.1875 to 0.1875
- key_matrix: bfloat16 [4096, 512], P(None, 'tp'), may hold values from -0.09375 to 0.09375
- value_matrix: bfloat16 [4096, 512], P(None, 'tp'), may hold values from -0.09375 to 0.09375
- output_weight: bfloat16 [4096, 4096], P('tp'), may hold values from -0.1875 to 0.1875
- document_bounds: int32 [9], replicated, may hold values from 0 to 2048, as said below
- block_owner: int32 [16], replicated, may hold values from 0 to 7, as said below
Outputs:
- attended: bfloat16 [2048, 4096], P('cp', 'tp')
Inputs may be any that keep to these rules, and one draw needn't show every extreme that they name: document_bounds[0] = 0, document_bounds[8] = 2048, strictly rising; document i holds the tokens from document_bounds[i] to document_bounds[i + 1] - 1. `block_owner`: every index of cp is named by exactly 2 blocks.
All inputs are finite; a program needn't handle non-finite values.
Results may differ from a plain program's by a relative error of at most 0.012.
The roundings to bfloat16 on the way count: a program that leaves them out, or rounds other values in their place, can miss the bound.
Values may be sent and summed in bfloat16 or wider, within the bound.
A program may use at most 128 MiB of HBM per device.

v0:
```python
import functools
import math

import jax
import jax.numpy as jnp
from jax import lax
from jax.experimental import pallas as pl
from jax.experimental.pallas import tpu as pltpu
from jax.sharding import PartitionSpec as P

HEAD_WIDTH = 128
BLOCK = 128


rope_theta = 500000.0
rope_factor = 8.0
rope_context = 8192.0
masked_score = -1e30


def rope_inverse(head_size):
    halves = jnp.arange(head_size // 2, dtype=jnp.float32)
    inverse = 1.0 / rope_theta ** (2.0 * halves / head_size)
    wavelength = 2.0 * math.pi / inverse
    smooth = (rope_context / wavelength - 1.0) / 3.0
    blended = (1.0 - smooth) * inverse / rope_factor + smooth * inverse
    longer = jnp.where(wavelength > rope_context, inverse / rope_factor, blended)
    return jnp.where(wavelength < rope_context / 4.0, inverse, longer)


def document_of(tokens, bounds):
    inner_bounds = bounds[1:-1]
    return jnp.sum((tokens[:, None] >= inner_bounds[None, :]).astype(jnp.int32), axis=1)


def position_of(tokens, bounds):
    starts = bounds[:-1]
    document_start = jnp.max(
        jnp.where(starts[None, :] <= tokens[:, None], starts[None, :], 0), axis=1
    )
    return tokens - document_start


def rotate(raw_rows, tokens, bounds, head_size):
    row_count = raw_rows.shape[0]
    head_count = raw_rows.shape[1] // head_size
    angles = (
        position_of(tokens, bounds).astype(jnp.float32)[:, None] * rope_inverse(head_size)[None, :]
    )
    cosine = jnp.cos(angles)[:, None, :]
    sine_table = jnp.sin(angles)[:, None, :]
    heads_view = raw_rows.reshape(row_count, head_count, head_size)
    front_half = heads_view[:, :, : head_size // 2]
    back_half = heads_view[:, :, head_size // 2 :]
    turned = jnp.concatenate(
        [
            front_half * cosine - back_half * sine_table,
            back_half * cosine + front_half * sine_table,
        ],
        axis=2,
    )
    return turned.reshape(row_count, head_count * head_size).astype(jnp.bfloat16)


def owner_order(block_owner, per_device):
    block_count = block_owner.shape[0]
    blocks = jnp.arange(block_count, dtype=jnp.int32)
    same_owner = block_owner[:, None] == block_owner[None, :]
    earlier = blocks[None, :] < blocks[:, None]
    owner_rank = jnp.sum((same_owner & earlier).astype(jnp.int32), axis=1)
    target = block_owner * per_device + owner_rank
    return jnp.sum(jnp.where(target[None, :] == blocks[:, None], blocks[None, :], 0), axis=1)


def relayout(local_rows, block_order):
    cp_size = lax.axis_size("cp")
    row_count, row_width = local_rows.shape
    per_device = row_count // BLOCK
    portion = BLOCK // cp_size
    pieces = local_rows.reshape(per_device, cp_size, portion * row_width)
    spread = lax.all_to_all(pieces, "cp", split_axis=1, concat_axis=0, tiled=True)
    spread = spread.reshape(per_device * cp_size, portion * row_width)
    wanted = block_order.reshape(cp_size, per_device).T.reshape(-1)
    outgoing = jnp.take(spread, wanted, axis=0).reshape(per_device, cp_size, portion * row_width)
    arrived = lax.all_to_all(outgoing, "cp", split_axis=1, concat_axis=1, tiled=True)
    return arrived.reshape(row_count, row_width)


def project(local_rows, query_weight, key_matrix, value_matrix):
    weight_list = (query_weight, key_matrix, value_matrix)
    portion = lax.all_gather(local_rows, "tp", axis=1, tiled=True)
    return tuple(
        (jnp.dot(portion, weight, preferred_element_type=jnp.float32) for weight in weight_list)
    )


def attend(queries, query_tokens, key_rows, value_rows, key_tokens, bounds, head_size, kv_heads):
    row_count = queries.shape[0]
    query_group_width = queries.shape[1] // (kv_heads * head_size)
    grouped = queries.reshape(row_count, kv_heads, query_group_width, head_size).transpose(
        1, 2, 0, 3
    )
    grouped = grouped.reshape(kv_heads, query_group_width * row_count, head_size)
    query_documents = document_of(query_tokens, bounds)
    score_scale = 1.0 / math.sqrt(head_size)

    def update(flash_state, key_block, value_block, token_block):
        block_rows = key_block.shape[0]
        key_documents = document_of(token_block, bounds)
        allowed = (query_documents[:, None] == key_documents[None, :]) & (
            token_block[None, :] <= query_tokens[:, None]
        )
        running_max, running_sum, running_out = flash_state
        per_head_keys = key_block.reshape(block_rows, kv_heads, head_size).transpose(1, 0, 2)
        per_head_values = value_block.reshape(block_rows, kv_heads, head_size).transpose(1, 0, 2)
        scores = (
            jnp.einsum("khd,ksd->khs", grouped, per_head_keys, preferred_element_type=jnp.float32)
            * score_scale
        )
        wide_mask = jnp.tile(allowed, (query_group_width, 1))[None, :, :]
        scores = jnp.where(wide_mask, scores, masked_score)
        new_max = jnp.maximum(running_max, jnp.max(scores, axis=2))
        weights = jnp.where(wide_mask, jnp.exp(scores - new_max[:, :, None]), 0.0)
        factor = jnp.exp(running_max - new_max)
        new_sum = running_sum * factor + jnp.sum(weights, axis=2)
        new_out = running_out * factor[:, :, None] + jnp.einsum(
            "khs,ksd->khd",
            weights.astype(jnp.bfloat16),
            per_head_values,
            preferred_element_type=jnp.float32,
        )
        return (new_max, new_sum, new_out)

    initial = (
        jnp.full((kv_heads, query_group_width * row_count), masked_score, jnp.float32),
        jnp.zeros((kv_heads, query_group_width * row_count), jnp.float32),
        jnp.zeros((kv_heads, query_group_width * row_count, head_size), jnp.float32),
    )
    key_part = lax.all_gather(key_rows, "cp", axis=0, tiled=True)
    value_part = lax.all_gather(value_rows, "cp", axis=0, tiled=True)
    token_part = lax.all_gather(key_tokens, "cp", axis=0, tiled=True)
    part_rows = key_part.shape[0]
    block_rows = math.gcd(part_rows, 512)

    def one_block(block_index, inner_state):
        first_row = block_index * block_rows
        return update(
            inner_state,
            lax.dynamic_slice_in_dim(key_part, first_row, block_rows, 0),
            lax.dynamic_slice_in_dim(value_part, first_row, block_rows, 0),
            lax.dynamic_slice_in_dim(token_part, first_row, block_rows, 0),
        )

    final_max, final_sum, final_out = lax.fori_loop(0, part_rows // block_rows, one_block, initial)
    normalized = final_out / final_sum[:, :, None]
    merged = normalized.reshape(kv_heads, query_group_width, row_count, head_size).transpose(
        2, 0, 1, 3
    )
    return merged.reshape(row_count, kv_heads * query_group_width * head_size).astype(jnp.bfloat16)


def output_rows(heads_out, output_weight):
    head_terms = jnp.dot(heads_out, output_weight, preferred_element_type=jnp.float32)
    return lax.psum_scatter(head_terms.astype(jnp.bfloat16), "tp", scatter_dimension=1, tiled=True)


MESH = pl.DeviceIdType.MESH
WINDOW = 512


def dot(a, b):
    return jnp.dot(a, b, preferred_element_type=jnp.float32)


def turn(raw, cosine, sine):
    half = raw.shape[1] // 2
    swapped = jnp.concatenate([raw[:, half:], raw[:, :half]], axis=1)
    return (raw * cosine + swapped * sine).astype(jnp.bfloat16)


def greet(n_cp, n_tp):
    c, z = lax.axis_index("cp"), lax.axis_index("tp")
    barrier = pltpu.get_barrier_semaphore()
    for t in range(1, n_cp):
        peer = lax.rem(c + t, n_cp)
        pl.semaphore_signal(barrier, inc=1, device_id={"cp": peer}, device_id_type=MESH)
    for t in range(1, n_tp):
        peer = lax.rem(z + t, n_tp)
        pl.semaphore_signal(barrier, inc=1, device_id={"tp": peer}, device_id_type=MESH)
    pl.semaphore_wait(barrier, n_cp + n_tp - 2)


def row_tokens(bounds, blocks, share, offset):
    shape = (blocks, share, HEAD_WIDTH)
    token = (
        lax.broadcasted_iota(jnp.int32, shape, 0) * BLOCK
        + lax.broadcasted_iota(jnp.int32, shape, 1) + offset
    )
    start = jnp.zeros_like(token)
    for i in range(bounds.shape[0] - 1):
        start = jnp.where(token >= bounds[i], bounds[i], start)
    return token, start


def project_kernel(
    n_cp, n_tp,
    bounds, hidden, wq_hbm, wk_hbm, wv_hbm, inverse,
    q_out, kv_out,
    rows, wq, wkv, acc_q, acc_kv, kv_own, kv_all, cosine, sine,
    w_sem, own_sem, s_send, s_recv, r_send, l_send, z_recv, k_send, k_recv, d_send, d_recv,
):
    c, z = lax.axis_index("cp"), lax.axis_index("tp")
    per = hidden.shape[0]
    width = hidden.shape[3]
    weights = (
        pltpu.make_async_copy(wq_hbm, wq, w_sem.at[0]),
        pltpu.make_async_copy(wk_hbm, wkv.at[:, pl.ds(0, HEAD_WIDTH)], w_sem.at[1]),
        pltpu.make_async_copy(wv_hbm, wkv.at[:, pl.ds(HEAD_WIDTH, HEAD_WIDTH)], w_sem.at[2]),
    )
    own = pltpu.make_async_copy(hidden.at[:, c], rows.at[z, pl.ds(c * per, per)], own_sem)
    own.start()
    greet(n_cp, n_tp)

    def spread(t):
        peer = lax.rem(c + t, n_cp)
        return pltpu.make_async_remote_copy(
            src_ref=hidden.at[:, peer], dst_ref=rows.at[z, pl.ds(c * per, per)],
            send_sem=s_send.at[t], recv_sem=s_recv.at[t],
            device_id={"cp": peer}, device_id_type=MESH,
        )

    def along(origin, t, step):
        source = lax.rem(c - t + n_cp, n_cp)
        piece = rows.at[origin, pl.ds(source * per, per)]
        sems = r_send if step > 0 else l_send
        return pltpu.make_async_remote_copy(
            src_ref=piece, dst_ref=piece,
            send_sem=sems.at[origin, t], recv_sem=z_recv.at[origin, t],
            device_id={"tp": lax.rem(z + step + n_tp, n_tp)}, device_id_type=MESH,
        )

    def multiply(origin, first):
        block = rows[origin].reshape(-1, width)
        span = pl.ds(pl.multiple_of(origin * width, width), width)
        kv_term = dot(block, wkv[span, :])
        q_term = dot(block, wq[span, :])
        if first:
            acc_kv[...] = kv_term
            acc_q[...] = q_term
        else:
            acc_kv[...] += kv_term
            acc_q[...] += q_term

    for t in range(1, n_cp):
        spread(t).start()
    for copy in weights:
        copy.start()
    for t in range(n_cp):
        if t == 0:
            own.wait()
        else:
            spread(t).wait_recv()

        @pl.when(z < n_tp - 1)
        def _():
            along(z, t, 1).start()

        @pl.when(z > 0)
        def _():
            along(z, t, -1).start()

    blocks, share = kv_own.shape[0], kv_own.shape[1]
    token, start = row_tokens(bounds, blocks, share, c * share)
    angle = (token - start).astype(jnp.float32).reshape(-1, HEAD_WIDTH) * inverse[...]
    cosine[...] = jnp.cos(angle)
    lane = lax.broadcasted_iota(jnp.int32, angle.shape, 1)
    sine[...] = jnp.where(lane < HEAD_WIDTH // 2, -1.0, 1.0) * jnp.sin(angle)
    for copy in weights:
        copy.wait()
    multiply(z, True)

    @pl.loop(1, n_tp - 1)
    def _(s):
        for t in range(n_cp):
            @pl.when(z - s >= 0)
            def _():
                along(z - s, t, 1).wait_recv()

                @pl.when(z < n_tp - 1)
                def _():
                    along(z - s, t, 1).start()

            @pl.when(z + s < n_tp)
            def _():
                along(z + s, t, -1).wait_recv()

                @pl.when(z > 0)
                def _():
                    along(z + s, t, -1).start()

        @pl.when(z - s >= 0)
        def _():
            multiply(z - s, False)

        @pl.when(z + s < n_tp)
        def _():
            multiply(z + s, False)

    chips = n_cp // 2
    partner = c + 1 - 2 * lax.rem(c, 2)
    count = per * share
    far = n_tp - 1 - z
    last = (z == 0) | (z == n_tp - 1)
    far_span = pl.ds(pl.multiple_of(far * width, width), width)

    def part_of(t):
        return lax.rem(c - t + n_cp, n_cp)

    def across(i, t):
        span = pl.ds(part_of(t) * per, per)
        return pltpu.make_async_remote_copy(
            src_ref=kv_own.at[span], dst_ref=kv_all.at[span, c],
            send_sem=k_send.at[i, t], recv_sem=k_recv.at[i, t],
            device_id={"cp": lax.rem(c + 2 * i, n_cp)}, device_id_type=MESH,
        )

    def arrived(i, t):
        source = lax.rem(c - 2 * i + n_cp, n_cp)
        span = pl.ds(lax.rem(source - t + n_cp, n_cp) * per, per)
        landed = kv_all.at[span, source]
        return pltpu.make_async_remote_copy(
            src_ref=landed, dst_ref=landed,
            send_sem=d_send.at[i, t], recv_sem=d_recv.at[i, t],
            device_id={"cp": partner}, device_id_type=MESH,
        )

    def handed(t):
        span = pl.ds(part_of(t) * per, per)
        return pltpu.make_async_remote_copy(
            src_ref=kv_own.at[span], dst_ref=kv_all.at[span, c],
            send_sem=d_send.at[0, t], recv_sem=d_recv.at[0, t],
            device_id={"cp": partner}, device_id_type=MESH,
        )

    @pl.loop(0, n_cp)
    def _(t):
        span = pl.ds(part_of(t) * per, per)
        lines = pl.ds(pl.multiple_of(part_of(t) * count, count), count)

        @pl.when(last)
        def _():
            along(far, t, 1).wait_recv()
            block = rows[far, span].reshape(count, width)
            acc_kv[lines, :] += dot(block, wkv[far_span, :])

        cos_t, sin_t = cosine[lines, :], sine[lines, :]
        key = turn(acc_kv[lines, :HEAD_WIDTH], cos_t, sin_t)
        value = acc_kv[lines, HEAD_WIDTH:].astype(jnp.bfloat16)
        tile = jnp.concatenate([key, value], axis=1).reshape(per, share, 2 * HEAD_WIDTH)
        kv_own[span] = tile
        kv_all[span, pl.ds(c, 1)] = tile[:, None]
        for i in range(1, chips):
            across(i, t).start()
        handed(t).start()

        @pl.when(last)
        def _():
            block = rows[far, span].reshape(count, width)
            acc_q[lines, :] += dot(block, wq[far_span, :])

        for h in range(q_out.shape[1] // HEAD_WIDTH):
            cols = slice(h * HEAD_WIDTH, (h + 1) * HEAD_WIDTH)
            q_out[lines, cols] = turn(acc_q[lines, cols], cos_t, sin_t)

    @pl.loop(0, n_cp)
    def _(t):
        for i in range(1, chips):
            across(i, t).wait_recv()
            arrived(i, t).start()

    @pl.loop(0, n_cp)
    def _(t):
        handed(t).wait_recv()
        for i in range(1, chips):
            arrived(i, t).wait_recv()

    kv_out[...] = kv_all[...]
    for t in range(1, n_cp):
        spread(t).wait_send()
    for t in range(n_cp):
        for o in range(n_tp):
            @pl.when((z < n_tp - 1) & (o <= z))
            def _():
                along(o, t, 1).wait_send()

            @pl.when((z > 0) & (o >= z))
            def _():
                along(o, t, -1).wait_send()

    @pl.loop(0, n_cp)
    def _(t):
        handed(t).wait_send()
        for i in range(1, chips):
            across(i, t).wait_send()
            arrived(i, t).wait_send()


def project_call(bounds, hidden, wq, wk, wv, inverse, n_cp, n_tp):
    rows, width = hidden.shape
    per = rows // BLOCK
    share = BLOCK // n_cp
    blocks = per * n_cp
    pieces = hidden.reshape(per, n_cp, share, width)
    bf, dma = jnp.bfloat16, pltpu.SemaphoreType.DMA
    vmem = pl.BlockSpec(memory_space=pltpu.VMEM)
    hbm = pl.BlockSpec(memory_space=pltpu.HBM)
    smem = pl.BlockSpec(memory_space=pltpu.SMEM)
    flops = 2 * rows * wq.shape[0] * (wq.shape[1] + 2 * HEAD_WIDTH)
    return pl.pallas_call(
        functools.partial(project_kernel, n_cp, n_tp),
        out_shape=(
            jax.ShapeDtypeStruct((rows, wq.shape[1]), bf),
            jax.ShapeDtypeStruct((blocks, n_cp, share, 2 * HEAD_WIDTH), bf),
        ),
        in_specs=[smem, hbm, hbm, hbm, hbm, vmem],
        out_specs=(vmem, vmem),
        scratch_shapes=[
            pltpu.VMEM((n_tp, blocks, share, width), bf),
            pltpu.VMEM(wq.shape, bf),
            pltpu.VMEM((wq.shape[0], 2 * HEAD_WIDTH), bf),
            pltpu.VMEM((rows, wq.shape[1]), jnp.float32),
            pltpu.VMEM((rows, 2 * HEAD_WIDTH), jnp.float32),
            pltpu.VMEM((blocks, share, 2 * HEAD_WIDTH), bf),
            pltpu.VMEM((blocks, n_cp, share, 2 * HEAD_WIDTH), bf),
            pltpu.VMEM((rows, HEAD_WIDTH), jnp.float32),
            pltpu.VMEM((rows, HEAD_WIDTH), jnp.float32),
            dma((3,)), dma, dma((n_cp,)), dma((n_cp,)),
            dma((n_tp, n_cp)), dma((n_tp, n_cp)), dma((n_tp, n_cp)),
            dma((n_cp // 2, n_cp)), dma((n_cp // 2, n_cp)),
            dma((n_cp // 2, n_cp)), dma((n_cp // 2, n_cp)),
        ],
        compiler_params=pltpu.CompilerParams(
            collective_id=1, has_side_effects=True, vmem_limit_bytes=48 << 20
        ),
        cost_estimate=pl.CostEstimate(flops=flops, bytes_accessed=12 << 20, transcendentals=0),
    )(bounds, pieces, wq, wk, wv, inverse)


def attend_kernel(bounds, owner, q_ref, kv_ref, out_ref, starts, tokens, where, *, heads, per):
    blocks, share = q_ref.shape[0], q_ref.shape[1]
    offset = lax.axis_index("cp") * share
    factor_of = math.log2(math.e) / math.sqrt(HEAD_WIDTH)
    keys = kv_ref.shape[0]
    window = min(WINDOW, keys)
    token_all, start_all = row_tokens(bounds, blocks, share, offset)
    tokens[...] = token_all
    starts[...] = start_all
    for d in range(blocks // per):
        where[blocks + d] = d * per
    for b in range(blocks):
        slot = where[blocks + owner[b]]
        where[b] = slot
        where[blocks + owner[b]] = slot + 1

    def stack(tile):
        return jnp.concatenate(
            [tile[:, h * HEAD_WIDTH : (h + 1) * HEAD_WIDTH] for h in range(heads)], axis=0
        )

    def scored(q, begin, stop, start, token):
        span = pl.ds(pl.multiple_of(begin, BLOCK), window)
        key = kv_ref[span, :HEAD_WIDTH]
        value = kv_ref[span, HEAD_WIDTH:]
        score = lax.dot_general(
            q, key, (((1,), (1,)), ((), ())), preferred_element_type=jnp.float32
        )
        index = begin + lax.broadcasted_iota(jnp.int32, score.shape, 1)
        allowed = (index >= start) & (index <= token)
        if stop is not None:
            allowed = allowed & (index < stop)
        return jnp.where(allowed, score, masked_score), value

    def one(b):
        q = stack(q_ref[b])
        start = jnp.tile(starts[b], (heads, 1))[:, :1]
        token = jnp.tile(tokens[b], (heads, 1))[:, :1]
        begin = jnp.maximum((b + 1) * BLOCK - window, 0)
        score, value = scored(q, begin, None, start, token)
        top = jnp.max(score, axis=1, keepdims=True)
        weight = jnp.exp2((score - top) * factor_of)
        total = jnp.sum(weight, axis=1, keepdims=True)
        out = dot(weight.astype(jnp.bfloat16), value)
        low = jnp.int32(0)
        for i in range(bounds.shape[0] - 1):
            low = jnp.where(b * BLOCK + offset >= bounds[i], bounds[i], low)

        def more(carry):
            stop, top, total, out = carry
            begin = jnp.maximum(stop - window, 0)
            score, value = scored(q, begin, stop, start, token)
            new_top = jnp.maximum(top, jnp.max(score, axis=1, keepdims=True))
            weight = jnp.exp2((score - new_top) * factor_of)
            factor = jnp.exp2((top - new_top) * factor_of)
            total = total * factor + jnp.sum(weight, axis=1, keepdims=True)
            out = out * factor + dot(weight.astype(jnp.bfloat16), value)
            return begin, new_top, total, out

        return low, more, (begin, top, total, out)

    group = 4

    @pl.loop(0, blocks // group)
    def _(g):
        firsts = [one(g * group + i) for i in range(group)]
        for i, (low, more, carry) in enumerate(firsts):
            _, _, total, out = lax.while_loop(lambda state: state[0] > low, more, carry)
            out = (out / total).astype(jnp.bfloat16)
            tile = jnp.concatenate(
                [out[h * share : (h + 1) * share] for h in range(heads)], axis=1
            )
            out_ref[where[g * group + i]] = tile


def attend_call(bounds, owner, q, kv, n_cp):
    rows, width = q.shape
    share = BLOCK // n_cp
    blocks = rows // share
    vmem = pl.BlockSpec(memory_space=pltpu.VMEM)
    smem = pl.BlockSpec(memory_space=pltpu.SMEM)
    return pl.pallas_call(
        functools.partial(attend_kernel, heads=width // HEAD_WIDTH, per=blocks // n_cp),
        out_shape=jax.ShapeDtypeStruct((blocks, share, width), jnp.bfloat16),
        in_specs=[smem, smem, vmem, vmem],
        out_specs=vmem,
        scratch_shapes=[
            pltpu.VMEM((blocks, share, HEAD_WIDTH), jnp.int32),
            pltpu.VMEM((blocks, share, HEAD_WIDTH), jnp.int32),
            pltpu.SMEM((blocks + n_cp,), jnp.int32),
        ],
        compiler_params=pltpu.CompilerParams(vmem_limit_bytes=32 << 20),
    )(bounds, owner, q.reshape(blocks, share, width), kv.reshape(-1, 2 * HEAD_WIDTH))


def output_kernel(
    n_cp, n_tp, heads, wo_hbm, out_ref,
    wo, part, from_left, from_right, to_right, to_left, done, landed,
    w_sem, r_send, l_send, r_recv, l_recv, a_send, a_recv,
):
    c, z = lax.axis_index("cp"), lax.axis_index("tp")
    per = out_ref.shape[0]
    share, width = heads.shape[1], out_ref.shape[3]

    def weight(o):
        cols = pl.ds(pl.multiple_of(o * width, width), width)
        return pltpu.make_async_copy(wo_hbm.at[:, cols], wo.at[o], w_sem.at[o])

    for s in range(n_tp - 1, -1, -1):
        @pl.when(z + s < n_tp)
        def _():
            weight(z + s).start()

        if s > 0:
            @pl.when(z - s >= 0)
            def _():
                weight(z - s).start()

    greet(n_cp, n_tp)

    def piece(t):
        return pl.ds(lax.rem(c + t, n_cp) * per, per)

    def rightward(o, t):
        return pltpu.make_async_remote_copy(
            src_ref=to_right.at[o, piece(t)], dst_ref=from_left.at[o, piece(t)],
            send_sem=r_send.at[o, t], recv_sem=r_recv.at[o, t],
            device_id={"tp": lax.rem(z + 1, n_tp)}, device_id_type=MESH,
        )

    def leftward(o, t):
        return pltpu.make_async_remote_copy(
            src_ref=to_left.at[o, piece(t)], dst_ref=from_right.at[o, piece(t)],
            send_sem=l_send.at[o, t], recv_sem=l_recv.at[o, t],
            device_id={"tp": lax.rem(z + n_tp - 1, n_tp)}, device_id_type=MESH,
        )

    def final(t):
        peer = lax.rem(c + t, n_cp)
        return pltpu.make_async_remote_copy(
            src_ref=done.at[piece(t)], dst_ref=landed.at[:, c],
            send_sem=a_send.at[t], recv_sem=a_recv.at[t],
            device_id={"cp": peer}, device_id_type=MESH,
        )

    def term(o):
        weight(o).wait()
        block = heads[...].reshape(-1, heads.shape[2])
        return dot(block, wo[o]).reshape(part.shape[1:])

    order = list(range(1, n_cp)) + [0]

    @pl.loop(0, n_tp - 1)
    def _(i):
        s = n_tp - 1 - i

        @pl.when(z + s < n_tp)
        def _():
            product = term(z + s)

            @pl.when(z == 0)
            def _():
                to_right[z + s] = product.astype(jnp.bfloat16)
                for t in order:
                    rightward(z + s, t).start()

            @pl.when(z > 0)
            def _():
                part[z + s] = product

        @pl.when(z - s >= 0)
        def _():
            product = term(z - s)

            @pl.when(z == n_tp - 1)
            def _():
                to_left[z - s] = product.astype(jnp.bfloat16)
                for t in order:
                    leftward(z - s, t).start()

            @pl.when(z < n_tp - 1)
            def _():
                part[z - s] = product

    part[z] = term(z)

    @pl.loop(0, n_tp - 1)
    def _(i):
        s = n_tp - 1 - i
        for t in order:
            @pl.when((z + s < n_tp) & (z > 0))
            def _():
                rightward(z + s, t).wait_recv()
                total = part[z + s, piece(t)] + from_left[z + s, piece(t)].astype(jnp.float32)
                to_right[z + s, piece(t)] = total.astype(jnp.bfloat16)
                rightward(z + s, t).start()

            @pl.when((z - s >= 0) & (z < n_tp - 1))
            def _():
                leftward(z - s, t).wait_recv()
                total = part[z - s, piece(t)] + from_right[z - s, piece(t)].astype(jnp.float32)
                to_left[z - s, piece(t)] = total.astype(jnp.bfloat16)
                leftward(z - s, t).start()

    for t in order:
        @pl.when(z > 0)
        def _():
            rightward(z, t).wait_recv()
            part[z, piece(t)] += from_left[z, piece(t)].astype(jnp.float32)

        @pl.when(z < n_tp - 1)
        def _():
            leftward(z, t).wait_recv()
            part[z, piece(t)] += from_right[z, piece(t)].astype(jnp.float32)

        done[piece(t)] = part[z, piece(t)].astype(jnp.bfloat16)
        if t > 0:
            final(t).start()

    for t in range(1, n_cp):
        final(t).wait_recv()
        source = lax.rem(c - t + n_cp, n_cp)
        out_ref[:, pl.ds(source, 1)] = landed[:, pl.ds(source, 1)]
    out_ref[:, pl.ds(c, 1)] = done[piece(0)][:, None]
    for t in range(1, n_cp):
        final(t).wait_send()
    for t in range(n_cp):
        for o in range(n_tp):
            @pl.when(o > z)
            def _():
                rightward(o, t).wait_send()

            @pl.when(o < z)
            def _():
                leftward(o, t).wait_send()


def output_call(heads, wo, n_cp, n_tp):
    blocks, share, depth = heads.shape
    width = wo.shape[1] // n_tp
    per = blocks // n_cp
    bf, dma = jnp.bfloat16, pltpu.SemaphoreType.DMA
    vmem = pl.BlockSpec(memory_space=pltpu.VMEM)
    slab = (n_tp, blocks, share, width)
    out = pl.pallas_call(
        functools.partial(output_kernel, n_cp, n_tp),
        out_shape=jax.ShapeDtypeStruct((per, n_cp, share, width), bf),
        in_specs=[vmem, pl.BlockSpec(memory_space=pltpu.HBM)],
        out_specs=vmem,
        scratch_shapes=[
            pltpu.VMEM((n_tp, depth, width), bf),
            pltpu.VMEM(slab, jnp.float32),
            pltpu.VMEM(slab, bf), pltpu.VMEM(slab, bf), pltpu.VMEM(slab, bf), pltpu.VMEM(slab, bf),
            pltpu.VMEM(slab[1:], bf),
            pltpu.VMEM((per, n_cp, share, width), bf),
            dma((n_tp,)), dma((n_tp, n_cp)), dma((n_tp, n_cp)), dma((n_tp, n_cp)), dma((n_tp, n_cp)),
            dma((n_cp,)), dma((n_cp,)),
        ],
        compiler_params=pltpu.CompilerParams(
            collective_id=2, has_side_effects=True, vmem_limit_bytes=48 << 20
        ),
        cost_estimate=pl.CostEstimate(
            flops=2 * blocks * share * depth * wo.shape[1], bytes_accessed=12 << 20, transcendentals=0
        ),
    )(heads, wo)
    return out.reshape(per * n_cp * share, width)


def local_fused(
    hidden, query_weight, key_matrix, value_matrix, output_weight, document_bounds, block_owner
):
    n_cp, n_tp = lax.axis_size("cp"), lax.axis_size("tp")
    inverse = jnp.tile(rope_inverse(HEAD_WIDTH), 2)[None, :]
    q, kv = project_call(
        document_bounds, hidden, query_weight, key_matrix, value_matrix, inverse, n_cp, n_tp
    )
    heads = attend_call(document_bounds, block_owner, q, kv, n_cp)
    return output_call(heads, output_weight, n_cp, n_tp)


def local_plain(
    hidden, query_weight, key_matrix, value_matrix, output_weight, document_bounds, block_owner
):
    cp_index = lax.axis_index("cp")
    row_count = hidden.shape[0]
    per_device = row_count // BLOCK
    block_order = owner_order(block_owner, per_device)
    own_blocks = lax.dynamic_slice_in_dim(block_order, cp_index * per_device, per_device, 0)
    new_tokens = (
        own_blocks[:, None] * BLOCK + jnp.arange(BLOCK, dtype=jnp.int32)[None, :]
    ).reshape(-1)
    kv_heads = key_matrix.shape[1] // HEAD_WIDTH
    moved = relayout(hidden, block_order)
    query_raw, key_raw, value_raw = project(moved, query_weight, key_matrix, value_matrix)
    queries = rotate(query_raw, new_tokens, document_bounds, HEAD_WIDTH)
    key_rows = rotate(key_raw, new_tokens, document_bounds, HEAD_WIDTH)
    value_rows = value_raw.astype(jnp.bfloat16)
    heads_out = attend(
        queries, new_tokens, key_rows, value_rows, new_tokens, document_bounds, HEAD_WIDTH, kv_heads
    )
    return output_rows(heads_out, output_weight)


def solution(mesh):
    shares = BLOCK // mesh.shape["cp"]
    local = local_fused if shares % 16 == 0 else local_plain
    placed = (P("cp", "tp"), P(None, "tp"), P(None, "tp"), P(None, "tp"), P("tp", None), P(), P())
    return jax.shard_map(
        local, mesh=mesh, in_specs=placed, out_specs=P("cp", "tp"), check_vma=False
    )
```

profile of v0, /device:TPU:9, one launch (start us, length us, event | category | flops | bytes accessed | tf_op | source)
XLA Modules:
  0.0 101.4 jit_solution(15141212782689138113)
XLA Ops:
  0.0 0.0 copy-start.4
  0.0 0.0 copy-start.5
  0.0 0.1 broadcast_in_dim_tile.3.inverse
  0.1 0.0 copy-start
  0.1 1.2 %copy-done = bf16[4096,128]{1,0:T(8,128)(2,1)S(1)} copy-done((bf16[4096,128]{1,0:T(8,128)(2,1)S(1)}, bf16[4096,128]{1,0:T(8,128)(2,1)}, u32[]{:S(2)}) %copy-start) | copy-done | bytes 1048600
  1.3 0.0 copy-start.1
  1.3 1.2 %copy-done.1 = bf16[4096,128]{1,0:T(8,128)(2,1)S(1)} copy-done((bf16[4096,128]{1,0:T(8,128)(2,1)S(1)}, bf16[4096,128]{1,0:T(8,128)(2,1)}, u32[]{:S(2)}) %copy-start.1) | copy-done | bytes 1048600
  2.6 0.0 copy-start.2
  2.6 1.0 %copy-done.2 = bf16[256,1024]{1,0:T(8,128)(2,1)S(1)} copy-done((bf16[256,1024]{1,0:T(8,128)(2,1)S(1)}, bf16[256,1024]{1,0:T(8,128)(2,1)}, u32[]{:S(2)}) %copy-start.2) | copy-done | bytes 524312
  3.6 0.0 copy-start.3
  3.6 0.7 copy-done.3
  4.3 42.3 %shard_map.73 = (bf16[256,1024]{1,0:T(8,128)(2,1)S(1)}, bf16[16,8,16,256]{3,2,1,0:T(8,128)(2,1)S(1)}) custom-call(s32[9]{0:T(128)S(1)} %copy-done.3, bf16[2,8,16,1024]{3,2,1,0:T(8,128)(2,1)S(1)} %bitcast.6, bf16[4096,1024]{1,0:T(8,128)(2,1)} %wq_hbm.1, bf16[4096,128]{1,0:T(8,128)(2,1)S(1)} %copy-done, bf16[4096,128]{1,0:T(8,128)(2,1)S(1)} %copy-done.1, ...), custom_call_target="tpu_custom_call" | custom-call | flops 2684354560 | bytes 12582912 | tf_op jit(solution)/shard_map/pallas_call | solution.py:419
  46.6 0.0 copy-done.4
  46.6 0.0 copy-done.5
  46.6 6.5 %shard_map.74.heads = bf16[16,16,1024]{2,1,0:T(8,128)(2,1)S(1)} custom-call(s32[9]{0:T(128)S(1)} %copy-done.4, s32[16]{0:T(128)S(1)} %copy-done.5, bf16[16,16,1024]{2,1,0:T(8,128)(2,1)S(1)} %bitcast.7, bf16[2048,256]{1,0:T(8,128)(2,1)S(1)} %bitcast.5), custom_call_target="tpu_custom_call" | custom-call | tf_op jit(solution)/shard_map/pallas_call | solution.py:530
  53.1 47.5 %shard_map.75 = bf16[2,8,16,1024]{3,2,1,0:T(8,128)(2,1)S(1)} custom-call(bf16[16,16,1024]{2,1,0:T(8,128)(2,1)S(1)} %shard_map.74.heads, bf16[1024,4096]{1,0:T(8,128)(2,1)} %wo_hbm.1), custom_call_target="tpu_custom_call" | custom-call | flops 2147483648 | bytes 12582912 | tf_op jit(solution)/shard_map/pallas_call | solution.py:693
  100.6 0.8 copy.9
  (2 shorter events, 0.0 us)
Async XLA Ops:
  0.0 46.6 %copy-start.4 = (s32[9]{0:T(128)S(1)}, s32[9]{0:T(128)}, u32[]{:S(2)}) copy-start(s32[9]{0:T(128)} %bounds.3) | copy-start | bytes 112
  0.0 46.6 %copy-start.5 = (s32[16]{0:T(128)S(1)}, s32[16]{0:T(128)}, u32[]{:S(2)}) copy-start(s32[16]{0:T(128)} %owner.1) | copy-start | bytes 196
  0.1 1.2 %copy-start = (bf16[4096,128]{1,0:T(8,128)(2,1)S(1)}, bf16[4096,128]{1,0:T(8,128)(2,1)}, u32[]{:S(2)}) copy-start(bf16[4096,128]{1,0:T(8,128)(2,1)} %wk_hbm.1) | copy-start | bytes 3145732
  1.3 1.2 %copy-start.1 = (bf16[4096,128]{1,0:T(8,128)(2,1)S(1)}, bf16[4096,128]{1,0:T(8,128)(2,1)}, u32[]{:S(2)}) copy-start(bf16[4096,128]{1,0:T(8,128)(2,1)} %wv_hbm.1) | copy-start | bytes 3145732
  2.6 1.0 %copy-start.2 = (bf16[256,1024]{1,0:T(8,128)(2,1)S(1)}, bf16[256,1024]{1,0:T(8,128)(2,1)}, u32[]{:S(2)}) copy-start(bf16[256,1024]{1,0:T(8,128)(2,1)} %param.7) | copy-start | bytes 1572868
  3.6 0.7 copy-start.3
where the time goes:
time: 102 us; the launch traced here: 101 us
  Pallas kernels  96.3 us (94%)
  local copies, waits for them, and re-layouts  5.04 us (5%)
    pallas_call x1, Pallas kernels, output_call(): pl.pallas_call(functools.partial(output_kernel, n_cp, n_tp), out_shape=ja...  47.5 us
    pallas_call x1, Pallas kernels, project_call(): pl.pallas_call(functools.partial(project_kernel, n_cp, n_tp), out_shape=(...  42.3 us
    pallas_call x1, Pallas kernels, attend_call(): pl.pallas_call(functools.partial(attend_kernel, heads=width // HEAD_WIDTH...  6.49 us
    unnamed x13, local copies, waits for them, and re-layouts  4.95 us

commit v1 on v0

v1 whole, which is shorter than its diff:
```python
import functools
import math

import jax
import jax.numpy as jnp
from jax import lax
from jax.experimental import pallas as pl
from jax.experimental.pallas import tpu as pltpu
from jax.sharding import PartitionSpec as P

HEAD_WIDTH = 128
BLOCK = 128


rope_theta = 500000.0
rope_factor = 8.0
rope_context = 8192.0
masked_score = -1e30


def rope_inverse(head_size):
    halves = jnp.arange(head_size // 2, dtype=jnp.float32)
    inverse = 1.0 / rope_theta ** (2.0 * halves / head_size)
    wavelength = 2.0 * math.pi / inverse
    smooth = (rope_context / wavelength - 1.0) / 3.0
    blended = (1.0 - smooth) * inverse / rope_factor + smooth * inverse
    longer = jnp.where(wavelength > rope_context, inverse / rope_factor, blended)
    return jnp.where(wavelength < rope_context / 4.0, inverse, longer)


def document_of(tokens, bounds):
    inner_bounds = bounds[1:-1]
    return jnp.sum((tokens[:, None] >= inner_bounds[None, :]).astype(jnp.int32), axis=1)


def position_of(tokens, bounds):
    starts = bounds[:-1]
    document_start = jnp.max(
        jnp.where(starts[None, :] <= tokens[:, None], starts[None, :], 0), axis=1
    )
    return tokens - document_start


def rotate(raw_rows, tokens, bounds, head_size):
    row_count = raw_rows.shape[0]
    head_count = raw_rows.shape[1] // head_size
    angles = (
        position_of(tokens, bounds).astype(jnp.float32)[:, None] * rope_inverse(head_size)[None, :]
    )
    cosine = jnp.cos(angles)[:, None, :]
    sine_table = jnp.sin(angles)[:, None, :]
    heads_view = raw_rows.reshape(row_count, head_count, head_size)
    front_half = heads_view[:, :, : head_size // 2]
    back_half = heads_view[:, :, head_size // 2 :]
    turned = jnp.concatenate(
        [
            front_half * cosine - back_half * sine_table,
            back_half * cosine + front_half * sine_table,
        ],
        axis=2,
    )
    return turned.reshape(row_count, head_count * head_size).astype(jnp.bfloat16)


def owner_order(block_owner, per_device):
    block_count = block_owner.shape[0]
    blocks = jnp.arange(block_count, dtype=jnp.int32)
    same_owner = block_owner[:, None] == block_owner[None, :]
    earlier = blocks[None, :] < blocks[:, None]
    owner_rank = jnp.sum((same_owner & earlier).astype(jnp.int32), axis=1)
    target = block_owner * per_device + owner_rank
    return jnp.sum(jnp.where(target[None, :] == blocks[:, None], blocks[None, :], 0), axis=1)


def relayout(local_rows, block_order):
    cp_size = lax.axis_size("cp")
    row_count, row_width = local_rows.shape
    per_device = row_count // BLOCK
    portion = BLOCK // cp_size
    pieces = local_rows.reshape(per_device, cp_size, portion * row_width)
    spread = lax.all_to_all(pieces, "cp", split_axis=1, concat_axis=0, tiled=True)
    spread = spread.reshape(per_device * cp_size, portion * row_width)
    wanted = block_order.reshape(cp_size, per_device).T.reshape(-1)
    outgoing = jnp.take(spread, wanted, axis=0).reshape(per_device, cp_size, portion * row_width)
    arrived = lax.all_to_all(outgoing, "cp", split_axis=1, concat_axis=1, tiled=True)
    return arrived.reshape(row_count, row_width)


def project(local_rows, query_weight, key_matrix, value_matrix):
    weight_list = (query_weight, key_matrix, value_matrix)
    portion = lax.all_gather(local_rows, "tp", axis=1, tiled=True)
    return tuple(
        (jnp.dot(portion, weight, preferred_element_type=jnp.float32) for weight in weight_list)
    )


def attend(queries, query_tokens, key_rows, value_rows, key_tokens, bounds, head_size, kv_heads):
    row_count = queries.shape[0]
    query_group_width = queries.shape[1] // (kv_heads * head_size)
    grouped = queries.reshape(row_count, kv_heads, query_group_width, head_size).transpose(
        1, 2, 0, 3
    )
    grouped = grouped.reshape(kv_heads, query_group_width * row_count, head_size)
    query_documents = document_of(query_tokens, bounds)
    score_scale = 1.0 / math.sqrt(head_size)

    def update(flash_state, key_block, value_block, token_block):
        block_rows = key_block.shape[0]
        key_documents = document_of(token_block, bounds)
        allowed = (query_documents[:, None] == key_documents[None, :]) & (
            token_block[None, :] <= query_tokens[:, None]
        )
        running_max, running_sum, running_out = flash_state
        per_head_keys = key_block.reshape(block_rows, kv_heads, head_size).transpose(1, 0, 2)
        per_head_values = value_block.reshape(block_rows, kv_heads, head_size).transpose(1, 0, 2)
        scores = (
            jnp.einsum("khd,ksd->khs", grouped, per_head_keys, preferred_element_type=jnp.float32)
            * score_scale
        )
        wide_mask = jnp.tile(allowed, (query_group_width, 1))[None, :, :]
        scores = jnp.where(wide_mask, scores, masked_score)
        new_max = jnp.maximum(running_max, jnp.max(scores, axis=2))
        weights = jnp.where(wide_mask, jnp.exp(scores - new_max[:, :, None]), 0.0)
        factor = jnp.exp(running_max - new_max)
        new_sum = running_sum * factor + jnp.sum(weights, axis=2)
        new_out = running_out * factor[:, :, None] + jnp.einsum(
            "khs,ksd->khd",
            weights.astype(jnp.bfloat16),
            per_head_values,
            preferred_element_type=jnp.float32,
        )
        return (new_max, new_sum, new_out)

    initial = (
        jnp.full((kv_heads, query_group_width * row_count), masked_score, jnp.float32),
        jnp.zeros((kv_heads, query_group_width * row_count), jnp.float32),
        jnp.zeros((kv_heads, query_group_width * row_count, head_size), jnp.float32),
    )
    key_part = lax.all_gather(key_rows, "cp", axis=0, tiled=True)
    value_part = lax.all_gather(value_rows, "cp", axis=0, tiled=True)
    token_part = lax.all_gather(key_tokens, "cp", axis=0, tiled=True)
    part_rows = key_part.shape[0]
    block_rows = math.gcd(part_rows, 512)

    def one_block(block_index, inner_state):
        first_row = block_index * block_rows
        return update(
            inner_state,
            lax.dynamic_slice_in_dim(key_part, first_row, block_rows, 0),
            lax.dynamic_slice_in_dim(value_part, first_row, block_rows, 0),
            lax.dynamic_slice_in_dim(token_part, first_row, block_rows, 0),
        )

    final_max, final_sum, final_out = lax.fori_loop(0, part_rows // block_rows, one_block, initial)
    normalized = final_out / final_sum[:, :, None]
    merged = normalized.reshape(kv_heads, query_group_width, row_count, head_size).transpose(
        2, 0, 1, 3
    )
    return merged.reshape(row_count, kv_heads * query_group_width * head_size).astype(jnp.bfloat16)


def output_rows(heads_out, output_weight):
    head_terms = jnp.dot(heads_out, output_weight, preferred_element_type=jnp.float32)
    return lax.psum_scatter(head_terms.astype(jnp.bfloat16), "tp", scatter_dimension=1, tiled=True)


MESH = pl.DeviceIdType.MESH
VMEM_LIMIT = 62 << 20


def dot(a, b):
    return jnp.dot(a, b, preferred_element_type=jnp.float32)


def turn(raw, cosine, sine):
    half = raw.shape[1] // 2
    swapped = jnp.concatenate([raw[:, half:], raw[:, :half]], axis=1)
    return (raw * cosine + swapped * sine).astype(jnp.bfloat16)


def greet(n_cp, n_tp):
    c, z = lax.axis_index("cp"), lax.axis_index("tp")
    barrier = pltpu.get_barrier_semaphore()
    for t in range(1, n_cp):
        peer = lax.rem(c + t, n_cp)
        pl.semaphore_signal(barrier, inc=1, device_id={"cp": peer}, device_id_type=MESH)
    for t in range(1, n_tp):
        peer = lax.rem(z + t, n_tp)
        pl.semaphore_signal(barrier, inc=1, device_id={"tp": peer}, device_id_type=MESH)
    pl.semaphore_wait(barrier, n_cp + n_tp - 2)


def row_tokens(bounds, blocks, share, offset):
    shape = (blocks, share, HEAD_WIDTH)
    token = (
        lax.broadcasted_iota(jnp.int32, shape, 0) * BLOCK
        + lax.broadcasted_iota(jnp.int32, shape, 1) + offset
    )
    start = jnp.zeros_like(token)
    for i in range(bounds.shape[0] - 1):
        start = jnp.where(token >= bounds[i], bounds[i], start)
    return token, start


def fused_kernel(
    n_cp, n_tp,
    bounds, owner, hidden, wq_hbm, wk_hbm, wv_hbm, wo_hbm, inverse,
    out_ref,
    rows, w, wo, cosine, sine, tokens, starts, q_all, kv_own, kv_all,
    part, from_left, from_right, to_right, to_left, done, outgoing, landed, order,
    w_sem, o_sem, own_sem, s_send, s_recv, r_send, l_send, z_recv, k_send, k_recv,
    pr_send, pl_send, pr_recv, pl_recv, a_send, a_recv,
):
    c, z = lax.axis_index("cp"), lax.axis_index("tp")
    per, width = hidden.shape[0], hidden.shape[3]
    share = hidden.shape[2]
    count = per * share
    q_width = wq_hbm.shape[1]
    heads = q_width // HEAD_WIDTH
    end = n_tp - 1
    factor_of = math.log2(math.e) / math.sqrt(HEAD_WIDTH)
    weights = (
        pltpu.make_async_copy(wk_hbm, w.at[:, pl.ds(q_width, HEAD_WIDTH)], w_sem.at[1]),
        pltpu.make_async_copy(wv_hbm, w.at[:, pl.ds(q_width + HEAD_WIDTH, HEAD_WIDTH)], w_sem.at[2]),
        pltpu.make_async_copy(wq_hbm, w.at[:, pl.ds(0, q_width)], w_sem.at[0]),
    )

    def out_weight(o):
        return pltpu.make_async_copy(
            wo_hbm.at[:, pl.ds(o * width, width)], wo.at[o], o_sem.at[o]
        )

    own = pltpu.make_async_copy(hidden.at[:, c], rows.at[z, pl.ds(c * per, per)], own_sem)
    own.start()
    greet(n_cp, n_tp)

    def spread(i):
        peer = lax.rem(c + i, n_cp)
        return pltpu.make_async_remote_copy(
            src_ref=hidden.at[:, peer], dst_ref=rows.at[z, pl.ds(c * per, per)],
            send_sem=s_send.at[i], recv_sem=s_recv.at[i],
            device_id={"cp": peer}, device_id_type=MESH,
        )

    def along(origin, t, step):
        piece = rows.at[origin, pl.ds(t * per, per)]
        sems = r_send if step > 0 else l_send
        return pltpu.make_async_remote_copy(
            src_ref=piece, dst_ref=piece,
            send_sem=sems.at[origin, t], recv_sem=z_recv.at[origin, t],
            device_id={"tp": lax.rem(z + step + n_tp, n_tp)}, device_id_type=MESH,
        )

    def keys_to(i, t):
        span = pl.ds(t * per, per)
        return pltpu.make_async_remote_copy(
            src_ref=kv_own.at[span], dst_ref=kv_all.at[span, c],
            send_sem=k_send.at[i, t], recv_sem=k_recv.at[i, t],
            device_id={"cp": lax.rem(c + i, n_cp)}, device_id_type=MESH,
        )

    def rightward(o, t):
        return pltpu.make_async_remote_copy(
            src_ref=to_right.at[o, t], dst_ref=from_left.at[o, t],
            send_sem=pr_send.at[o, t], recv_sem=pr_recv.at[o, t],
            device_id={"tp": lax.rem(z + 1, n_tp)}, device_id_type=MESH,
        )

    def leftward(o, t):
        return pltpu.make_async_remote_copy(
            src_ref=to_left.at[o, t], dst_ref=from_right.at[o, t],
            send_sem=pl_send.at[o, t], recv_sem=pl_recv.at[o, t],
            device_id={"tp": lax.rem(z + n_tp - 1, n_tp)}, device_id_type=MESH,
        )

    def final(i):
        peer = lax.rem(c + i, n_cp)
        return pltpu.make_async_remote_copy(
            src_ref=outgoing.at[pl.ds(peer * per, per)], dst_ref=landed.at[:, c],
            send_sem=a_send.at[i], recv_sem=a_recv.at[i],
            device_id={"cp": peer}, device_id_type=MESH,
        )

    def outward(origin, t):
        @pl.when(z < end)
        def _():
            along(origin, t, 1).start()

        @pl.when(z > 0)
        def _():
            along(origin, t, -1).start()

    for i in range(1, n_cp):
        spread(i).start()
    for copy in weights:
        copy.start()
    for o in range(n_tp):
        out_weight(o).start()
    own.wait()
    outward(z, c)

    blocks = per * n_cp
    token, start = row_tokens(bounds, blocks, share, c * share)
    tokens[...] = token.reshape(-1, HEAD_WIDTH)
    starts[...] = start.reshape(-1, HEAD_WIDTH)
    angle = (token - start).astype(jnp.float32).reshape(-1, HEAD_WIDTH) * inverse[...]
    cosine[...] = jnp.cos(angle)
    lane = lax.broadcasted_iota(jnp.int32, angle.shape, 1)
    sine[...] = jnp.where(lane < HEAD_WIDTH // 2, -1.0, 1.0) * jnp.sin(angle)

    def gather(s):
        for d in range(n_tp):
            t = s + end - d

            @pl.when((t >= 0) & (t < n_cp))
            def _():
                if d == 0:
                    @pl.when(t != c)
                    def _():
                        spread(lax.rem(c - t + n_cp, n_cp)).wait_recv()
                        outward(z, t)
                else:
                    @pl.when(z - d >= 0)
                    def _():
                        along(z - d, t, 1).wait_recv()

                        @pl.when(z < end)
                        def _():
                            along(z - d, t, 1).start()

                    @pl.when(z + d < n_tp)
                    def _():
                        along(z + d, t, -1).wait_recv()

                        @pl.when(z > 0)
                        def _():
                            along(z + d, t, -1).start()

    def project(t):
        span = pl.ds(t * per, per)
        lines = pl.ds(pl.multiple_of(t * count, count), count)
        x = jnp.concatenate([rows[o, span].reshape(count, width) for o in range(n_tp)], axis=1)
        cos_t, sin_t = cosine[lines, :], sine[lines, :]
        raw = dot(x, w[:, q_width:])
        key = turn(raw[:, :HEAD_WIDTH], cos_t, sin_t)
        value = raw[:, HEAD_WIDTH:].astype(jnp.bfloat16)
        tile = jnp.concatenate([key, value], axis=1).reshape(per, share, 2 * HEAD_WIDTH)
        kv_own[span] = tile
        kv_all[span, pl.ds(c, 1)] = tile[:, None]
        for i in range(1, n_cp):
            keys_to(i, t).start()
        raw_q = dot(x, w[:, :q_width])
        for h in range(heads):
            q_all[t, h * count : (h + 1) * count] = turn(
                raw_q[:, h * HEAD_WIDTH : (h + 1) * HEAD_WIDTH], cos_t, sin_t
            )

    def attend(t):
        lines = pl.ds(pl.multiple_of(t * count, count), count)
        q = q_all[t]
        start = jnp.tile(starts[lines, :], (heads, 1))[:, :1]
        token = jnp.tile(tokens[lines, :], (heads, 1))[:, :1]
        keys = per * BLOCK

        def more(k, carry):
            top, total, out = carry
            u = t - k
            span = pl.ds(u * per, per)
            key = kv_all[span, :, :, :HEAD_WIDTH].reshape(keys, HEAD_WIDTH)
            value = kv_all[span, :, :, HEAD_WIDTH:].reshape(keys, HEAD_WIDTH)
            score = lax.dot_general(
                q, key, (((1,), (1,)), ((), ())), preferred_element_type=jnp.float32
            )
            index = u * keys + lax.broadcasted_iota(jnp.int32, score.shape, 1)
            score = jnp.where((index >= start) & (index <= token), score, masked_score)
            new_top = jnp.maximum(top, jnp.max(score, axis=1, keepdims=True))
            weight = jnp.exp2((score - new_top) * factor_of)
            factor = jnp.exp2((top - new_top) * factor_of)
            total = total * factor + jnp.sum(weight, axis=1, keepdims=True)
            out = out * factor + dot(weight.astype(jnp.bfloat16), value)
            return new_top, total, out

        lengths = (heads * count, 1)
        initial = (
            jnp.full(lengths, masked_score, jnp.float32),
            jnp.zeros(lengths, jnp.float32),
            jnp.zeros((heads * count, HEAD_WIDTH), jnp.float32),
        )
        _, total, out = lax.fori_loop(0, t + 1, more, initial)
        out = (out / total).astype(jnp.bfloat16)
        return jnp.concatenate([out[h * count : (h + 1) * count] for h in range(heads)], axis=1)

    def output(t, attended):
        high = z // (n_tp // 2)
        for k in range(n_tp):
            o = (1 - high) * (end - k) + high * k
            product = dot(attended, wo[o])
            go_right = (z == 0) & (o > z)
            go_left = (z == end) & (o < z)

            @pl.when(go_right)
            def _():
                to_right[o, t] = product.astype(jnp.bfloat16)
                rightward(o, t).start()

            @pl.when(go_left)
            def _():
                to_left[o, t] = product.astype(jnp.bfloat16)
                leftward(o, t).start()

            @pl.when(jnp.logical_not(go_right | go_left))
            def _():
                part[o, t] = product

    def reduce(s):
        t_right = s - 1 - z
        t_left = s - 1 - (end - z)

        @pl.when((z > 0) & (t_right >= 0) & (t_right < n_cp))
        def _():
            for o in range(end, 0, -1):
                @pl.when(o > z)
                def _():
                    rightward(o, t_right).wait_recv()
                    total = part[o, t_right] + from_left[o, t_right].astype(jnp.float32)
                    to_right[o, t_right] = total.astype(jnp.bfloat16)
                    rightward(o, t_right).start()

        @pl.when((z < end) & (t_left >= 0) & (t_left < n_cp))
        def _():
            for o in range(end):
                @pl.when(o < z)
                def _():
                    leftward(o, t_left).wait_recv()
                    total = part[o, t_left] + from_right[o, t_left].astype(jnp.float32)
                    to_left[o, t_left] = total.astype(jnp.bfloat16)
                    leftward(o, t_left).start()

    def finish(t):
        @pl.when(z > 0)
        def _():
            rightward(z, t).wait_recv()
            part[z, t] += from_left[z, t].astype(jnp.float32)

        @pl.when(z < end)
        def _():
            leftward(z, t).wait_recv()
            part[z, t] += from_right[z, t].astype(jnp.float32)

        done[pl.ds(t * per, per)] = part[z, t].astype(jnp.bfloat16).reshape(per, share, width)

    @pl.loop(0, n_cp + 2 * n_tp - 1)
    def _(step):
        s = step - end
        gather(s)
        reduce(s)

        @pl.when((s >= 0) & (s < n_cp))
        def _():
            @pl.when(s == 0)
            def _():
                for copy in weights:
                    copy.wait()

            project(s)

        @pl.when((s >= 1) & (s <= n_cp))
        def _():
            @pl.when(s == 1)
            def _():
                for o in range(n_tp):
                    out_weight(o).wait()

            for i in range(1, n_cp):
                keys_to(i, s - 1).wait_recv()
            output(s - 1, attend(s - 1))

        @pl.when(s >= n_tp)
        def _():
            finish(s - n_tp)

    for b in range(blocks):
        rank = jnp.int32(0)
        for e in range(b):
            rank += (owner[e] == owner[b]).astype(jnp.int32)
        order[b] = owner[b] * per + rank
    for b in range(blocks):
        def seek(e, found):
            return jnp.where(order[e] == b, e, found)
        source = lax.fori_loop(0, blocks, seek, jnp.int32(0))
        outgoing[b] = done[source]
    for i in range(1, n_cp):
        final(i).start()
    out_ref[:, pl.ds(c, 1)] = outgoing[pl.ds(c * per, per)][:, None]
    for i in range(1, n_cp):
        final(i).wait_recv()
        source = lax.rem(c - i + n_cp, n_cp)
        out_ref[:, pl.ds(source, 1)] = landed[:, pl.ds(source, 1)]
    for i in range(1, n_cp):
        spread(i).wait_send()
        final(i).wait_send()

    @pl.loop(0, n_cp)
    def _(t):
        for i in range(1, n_cp):
            keys_to(i, t).wait_send()
        for o in range(n_tp):
            @pl.when((z < end) & (o <= z))
            def _():
                along(o, t, 1).wait_send()

            @pl.when((z > 0) & (o >= z))
            def _():
                along(o, t, -1).wait_send()

            @pl.when(o > z)
            def _():
                rightward(o, t).wait_send()

            @pl.when(o < z)
            def _():
                leftward(o, t).wait_send()


def fused_call(bounds, owner, hidden, wq, wk, wv, wo, inverse, n_cp, n_tp):
    rows, width = hidden.shape
    per = rows // BLOCK
    share = BLOCK // n_cp
    blocks, count = per * n_cp, per * share
    heads = wq.shape[1] // HEAD_WIDTH
    pieces = hidden.reshape(per, n_cp, share, width)
    bf, f32, i32, dma = jnp.bfloat16, jnp.float32, jnp.int32, pltpu.SemaphoreType.DMA
    vmem = pl.BlockSpec(memory_space=pltpu.VMEM)
    hbm = pl.BlockSpec(memory_space=pltpu.HBM)
    smem = pl.BlockSpec(memory_space=pltpu.SMEM)
    slab = (n_tp, n_cp, count, width)
    kv_width = 2 * HEAD_WIDTH
    sems = dma((n_tp, n_cp))
    flops = 2 * rows * (wq.shape[0] * (wq.shape[1] + kv_width) + wo.shape[0] * wo.shape[1])
    out = pl.pallas_call(
        functools.partial(fused_kernel, n_cp, n_tp),
        out_shape=jax.ShapeDtypeStruct((per, n_cp, share, width), bf),
        in_specs=[smem, smem, hbm, hbm, hbm, hbm, hbm, vmem],
        out_specs=vmem,
        scratch_shapes=[
            pltpu.VMEM((n_tp, blocks, share, width), bf),
            pltpu.VMEM((wq.shape[0], wq.shape[1] + kv_width), bf),
            pltpu.VMEM((n_tp, wo.shape[0], width), bf),
            pltpu.VMEM((rows, HEAD_WIDTH), f32), pltpu.VMEM((rows, HEAD_WIDTH), f32),
            pltpu.VMEM((rows, HEAD_WIDTH), i32), pltpu.VMEM((rows, HEAD_WIDTH), i32),
            pltpu.VMEM((n_cp, heads * count, HEAD_WIDTH), bf),
            pltpu.VMEM((blocks, share, kv_width), bf),
            pltpu.VMEM((blocks, n_cp, share, kv_width), bf),
            pltpu.VMEM(slab, f32),
            pltpu.VMEM(slab, bf), pltpu.VMEM(slab, bf), pltpu.VMEM(slab, bf), pltpu.VMEM(slab, bf),
            pltpu.VMEM((blocks, share, width), bf),
            pltpu.VMEM((blocks, share, width), bf),
            pltpu.VMEM((per, n_cp, share, width), bf),
            pltpu.SMEM((blocks,), i32),
            dma((3,)), dma((n_tp,)), dma, dma((n_cp,)), dma((n_cp,)), sems, sems, sems,
            dma((n_cp, n_cp)), dma((n_cp, n_cp)),
            sems, sems, sems, sems, dma((n_cp,)), dma((n_cp,)),
        ],
        compiler_params=pltpu.CompilerParams(
            collective_id=1, has_side_effects=True, vmem_limit_bytes=VMEM_LIMIT
        ),
        cost_estimate=pl.CostEstimate(flops=flops, bytes_accessed=20 << 20, transcendentals=0),
    )(bounds, owner, pieces, wq, wk, wv, wo, inverse)
    return out.reshape(rows, width)


def local_fused(
    hidden, query_weight, key_matrix, value_matrix, output_weight, document_bounds, block_owner
):
    n_cp, n_tp = lax.axis_size("cp"), lax.axis_size("tp")
    inverse = jnp.tile(rope_inverse(HEAD_WIDTH), 2)[None, :]
    return fused_call(
        document_bounds, block_owner, hidden, query_weight, key_matrix, value_matrix,
        output_weight, inverse, n_cp, n_tp,
    )


def local_plain(
    hidden, query_weight, key_matrix, value_matrix, output_weight, document_bounds, block_owner
):
    cp_index = lax.axis_index("cp")
    row_count = hidden.shape[0]
    per_device = row_count // BLOCK
    block_order = owner_order(block_owner, per_device)
    own_blocks = lax.dynamic_slice_in_dim(block_order, cp_index * per_device, per_device, 0)
    new_tokens = (
        own_blocks[:, None] * BLOCK + jnp.arange(BLOCK, dtype=jnp.int32)[None, :]
    ).reshape(-1)
    kv_heads = key_matrix.shape[1] // HEAD_WIDTH
    moved = relayout(hidden, block_order)
    query_raw, key_raw, value_raw = project(moved, query_weight, key_matrix, value_matrix)
    queries = rotate(query_raw, new_tokens, document_bounds, HEAD_WIDTH)
    key_rows = rotate(key_raw, new_tokens, document_bounds, HEAD_WIDTH)
    value_rows = value_raw.astype(jnp.bfloat16)
    heads_out = attend(
        queries, new_tokens, key_rows, value_rows, new_tokens, document_bounds, HEAD_WIDTH, kv_heads
    )
    return output_rows(heads_out, output_weight)


def solution(mesh):
    shares = BLOCK // mesh.shape["cp"]
    local = local_fused if shares % 16 == 0 else local_plain
    placed = (P("cp", "tp"), P(None, "tp"), P(None, "tp"), P(None, "tp"), P("tp", None), P(), P())
    return jax.shard_map(
        local, mesh=mesh, in_specs=placed, out_specs=P("cp", "tp"), check_vma=False
    )
```

time: 102 us -> 103 us (level)
  the two profiles are of different devices: /device:TPU:9 before, /device:TPU:1 now
where the time goes in v1:
time: 103 us
  Pallas kernels  100 us (97%)
  local copies, waits for them, and re-layouts  2.47 us (2%)
    pallas_call x1, Pallas kernels, fused_call(): pl.pallas_call(functools.partial(fused_kernel, n_cp, n_tp), out_shape=jax...  100 us

profile of v1, /device:TPU:1, one launch (start us, length us, event | category | flops | bytes accessed | tf_op | source)
XLA Modules:
  0.0 102.8 jit_solution(18188380646766032467)
XLA Ops:
  0.0 0.6 broadcast_in_dim_tile.3.inverse
  0.6 100.3 %shard_map.73 = bf16[2,8,16,1024]{3,2,1,0:T(8,128)(2,1)} custom-call(s32[9]{0:T(128)} %bounds.1, s32[16]{0:T(128)} %owner.1, bf16[2,8,16,1024]{3,2,1,0:T(8,128)(2,1)} %bitcast.3, bf16[4096,1024]{1,0:T(8,128)(2,1)} %wq_hbm.1, bf16[4096,128]{1,0:T(8,128)(2,1)} %wk_hbm.1, bf16[4096,128]{1,0:T(8,128)(2,1)} %wv_hbm.1, bf16[1024,4096]{1,0:T(8,128)(2,1)} %wo_hbm.1, ...), custom_call_target="tpu_custom_call" | custom-call | flops 4831838208 | bytes 20971520 | tf_op jit(solution)/shard_map/pallas_call | solution.py:540
  100.9 1.9 %copy.9 = bf16[256,1024]{1,0:T(8,128)(2,1)} copy(bf16[256,1024]{1,0:T(8,128)(2,1)} %bitcast.2) | data formatting | bytes 1048576
  (2 shorter events, 0.0 us)

commit v2 on v1

--- a/solution.py
+++ b/solution.py
@@ -165,7 +165,7 @@
 
 
 MESH = pl.DeviceIdType.MESH
-VMEM_LIMIT = 62 << 20
+VMEM_LIMIT = 53 << 20
 
 
 def dot(a, b):
@@ -202,32 +202,40 @@
     return token, start
 
 
+def chunk_sizes(sources):
+    if sources < 4 or sources % 2:
+        return [1] * sources
+    return [1] + [2] * ((sources - 2) // 2) + [1]
+
+
 def fused_kernel(
-    n_cp, n_tp,
+    n_cp, n_tp, sizes,
     bounds, owner, hidden, wq_hbm, wk_hbm, wv_hbm, wo_hbm, inverse,
     out_ref,
     rows, w, wo, cosine, sine, tokens, starts, q_all, kv_own, kv_all,
     part, from_left, from_right, to_right, to_left, done, outgoing, landed, order,
-    w_sem, o_sem, own_sem, s_send, s_recv, r_send, l_send, z_recv, k_send, k_recv,
+    w_sem, o_sem, own_sem, s_send, s_recv, d_send, r_send, l_send, z_recv, k_send, k_recv,
     pr_send, pl_send, pr_recv, pl_recv, a_send, a_recv,
 ):
     c, z = lax.axis_index("cp"), lax.axis_index("tp")
-    per, width = hidden.shape[0], hidden.shape[3]
-    share = hidden.shape[2]
-    count = per * share
+    per, share, width = hidden.shape[0], hidden.shape[2], hidden.shape[3]
+    blocks = per * n_cp
+    unit = per * share
     q_width = wq_hbm.shape[1]
     heads = q_width // HEAD_WIDTH
     end = n_tp - 1
+    last = len(sizes)
+    firsts = [sum(sizes[:k]) for k in range(last + 1)]
     factor_of = math.log2(math.e) / math.sqrt(HEAD_WIDTH)
     weights = (
-        pltpu.make_async_copy(wk_hbm, w.at[:, pl.ds(q_width, HEAD_WIDTH)], w_sem.at[1]),
-        pltpu.make_async_copy(wv_hbm, w.at[:, pl.ds(q_width + HEAD_WIDTH, HEAD_WIDTH)], w_sem.at[2]),
-        pltpu.make_async_copy(wq_hbm, w.at[:, pl.ds(0, q_width)], w_sem.at[0]),
+        pltpu.make_async_copy(wk_hbm, w.at[:, pl.ds(q_width, HEAD_WIDTH)], w_sem),
+        pltpu.make_async_copy(wv_hbm, w.at[:, pl.ds(q_width + HEAD_WIDTH, HEAD_WIDTH)], w_sem),
+        pltpu.make_async_copy(wq_hbm, w.at[:, pl.ds(0, q_width)], w_sem),
     )
 
     def out_weight(o):
         return pltpu.make_async_copy(
-            wo_hbm.at[:, pl.ds(o * width, width)], wo.at[o], o_sem.at[o]
+            wo_hbm.at[:, pl.ds(o * width, width)], wo.at[o], o_sem
         )
 
     own = pltpu.make_async_copy(hidden.at[:, c], rows.at[z, pl.ds(c * per, per)], own_sem)
@@ -238,38 +246,51 @@
         peer = lax.rem(c + i, n_cp)
         return pltpu.make_async_remote_copy(
             src_ref=hidden.at[:, peer], dst_ref=rows.at[z, pl.ds(c * per, per)],
-            send_sem=s_send.at[i], recv_sem=s_recv.at[i],
+            send_sem=s_send, recv_sem=s_recv.at[i],
             device_id={"cp": peer}, device_id_type=MESH,
         )
 
-    def along(origin, t, step):
-        piece = rows.at[origin, pl.ds(t * per, per)]
+    def along(origin, source, step):
+        piece = rows.at[origin, pl.ds(source * per, per)]
         sems = r_send if step > 0 else l_send
         return pltpu.make_async_remote_copy(
             src_ref=piece, dst_ref=piece,
-            send_sem=sems.at[origin, t], recv_sem=z_recv.at[origin, t],
+            send_sem=sems, recv_sem=z_recv.at[origin, source],
             device_id={"tp": lax.rem(z + step + n_tp, n_tp)}, device_id_type=MESH,
         )
 
-    def keys_to(i, t):
-        span = pl.ds(t * per, per)
+    def skip(step):
+        piece = rows.at[z, pl.ds(0, per)]
         return pltpu.make_async_remote_copy(
-            src_ref=kv_own.at[span], dst_ref=kv_all.at[span, c],
-            send_sem=k_send.at[i, t], recv_sem=k_recv.at[i, t],
+            src_ref=piece, dst_ref=piece,
+            send_sem=d_send.at[(step + 1) // 2], recv_sem=z_recv.at[z, 0],
+            device_id={"tp": lax.rem(z + 2 * step + n_tp, n_tp)}, device_id_type=MESH,
+        )
+
+    def blocks_of(k):
+        return pl.ds(firsts[k] * per, sizes[k] * per)
+
+    def lines_of(k):
+        return pl.ds(firsts[k] * unit, sizes[k] * unit)
+
+    def keys_to(i, k):
+        return pltpu.make_async_remote_copy(
+            src_ref=kv_own.at[blocks_of(k)], dst_ref=kv_all.at[blocks_of(k), c],
+            send_sem=k_send, recv_sem=k_recv.at[k],
             device_id={"cp": lax.rem(c + i, n_cp)}, device_id_type=MESH,
         )
 
-    def rightward(o, t):
+    def rightward(o, k):
         return pltpu.make_async_remote_copy(
-            src_ref=to_right.at[o, t], dst_ref=from_left.at[o, t],
-            send_sem=pr_send.at[o, t], recv_sem=pr_recv.at[o, t],
+            src_ref=to_right.at[o, lines_of(k)], dst_ref=from_left.at[o, lines_of(k)],
+            send_sem=pr_send, recv_sem=pr_recv.at[o - 1, k],
             device_id={"tp": lax.rem(z + 1, n_tp)}, device_id_type=MESH,
         )
 
-    def leftward(o, t):
+    def leftward(o, k):
         return pltpu.make_async_remote_copy(
-            src_ref=to_left.at[o, t], dst_ref=from_right.at[o, t],
-            send_sem=pl_send.at[o, t], recv_sem=pl_recv.at[o, t],
+            src_ref=to_left.at[o, lines_of(k)], dst_ref=from_right.at[o, lines_of(k)],
+            send_sem=pl_send, recv_sem=pl_recv.at[o, k],
             device_id={"tp": lax.rem(z + n_tp - 1, n_tp)}, device_id_type=MESH,
         )
 
@@ -277,18 +298,9 @@
         peer = lax.rem(c + i, n_cp)
         return pltpu.make_async_remote_copy(
             src_ref=outgoing.at[pl.ds(peer * per, per)], dst_ref=landed.at[:, c],
-            send_sem=a_send.at[i], recv_sem=a_recv.at[i],
+            send_sem=a_send, recv_sem=a_recv,
             device_id={"cp": peer}, device_id_type=MESH,
         )
-
-    def outward(origin, t):
-        @pl.when(z < end)
-        def _():
-            along(origin, t, 1).start()
-
-        @pl.when(z > 0)
-        def _():
-            along(origin, t, -1).start()
 
     for i in range(1, n_cp):
         spread(i).start()
@@ -296,10 +308,7 @@
         copy.start()
     for o in range(n_tp):
         out_weight(o).start()
-    own.wait()
-    outward(z, c)
-
-    blocks = per * n_cp
+
     token, start = row_tokens(bounds, blocks, share, c * share)
     tokens[...] = token.reshape(-1, HEAD_WIDTH)
     starts[...] = start.reshape(-1, HEAD_WIDTH)
@@ -307,238 +316,350 @@
     cosine[...] = jnp.cos(angle)
     lane = lax.broadcasted_iota(jnp.int32, angle.shape, 1)
     sine[...] = jnp.where(lane < HEAD_WIDTH // 2, -1.0, 1.0) * jnp.sin(angle)
-
-    def gather(s):
-        for d in range(n_tp):
-            t = s + end - d
-
-            @pl.when((t >= 0) & (t < n_cp))
+    slots = []
+    for b in range(blocks):
+        rank = jnp.int32(0)
+        for e in range(b):
+            rank += (owner[e] == owner[b]).astype(jnp.int32)
+        slots.append(owner[b] * per + rank)
+    for b in range(blocks):
+        found = jnp.int32(0)
+        for e in range(1, blocks):
+            found = jnp.where(slots[e] == b, e, found)
+        order[b] = found
+    own.wait()
+
+    inner = (z > 0) & (z < end)
+
+    def take(source):
+        @pl.when(source != c)
+        def _():
+            spread(lax.rem(c - source + n_cp, n_cp)).wait_recv()
+
+    def end_sends(source):
+        @pl.when(z == 0)
+        def _():
+            along(z, source, 1).start()
+
+        @pl.when(z == end)
+        def _():
+            along(z, source, -1).start()
+
+    def first_sends():
+        for step in (1, -1):
+            @pl.when((z + step >= 0) & (z + step < n_tp))
             def _():
-                if d == 0:
-                    @pl.when(t != c)
-                    def _():
-                        spread(lax.rem(c - t + n_cp, n_cp)).wait_recv()
-                        outward(z, t)
-                else:
-                    @pl.when(z - d >= 0)
-                    def _():
-                        along(z - d, t, 1).wait_recv()
-
-                        @pl.when(z < end)
+                along(z, 0, step).start()
+
+            @pl.when((z + 2 * step >= 0) & (z + 2 * step < n_tp))
+            def _():
+                skip(step).start()
+
+    def first_waits():
+        for d in range(1, n_tp):
+            for step in (1, -1):
+                @pl.when((z - step * d >= 0) & (z - step * d < n_tp))
+                def _():
+                    along(z - step * d, 0, step).wait_recv()
+                    if d > 1:
+                        @pl.when((z + step >= 0) & (z + step < n_tp))
                         def _():
-                            along(z - d, t, 1).start()
-
-                    @pl.when(z + d < n_tp)
-                    def _():
-                        along(z + d, t, -1).wait_recv()
-
-                        @pl.when(z > 0)
-                        def _():
-                            along(z + d, t, -1).start()
-
-    def project(t):
-        span = pl.ds(t * per, per)
-        lines = pl.ds(pl.multiple_of(t * count, count), count)
-        x = jnp.concatenate([rows[o, span].reshape(count, width) for o in range(n_tp)], axis=1)
-        cos_t, sin_t = cosine[lines, :], sine[lines, :]
+                            along(z - step * d, 0, step).start()
+
+    def end_waits(source):
+        for d in range(1, n_tp):
+            @pl.when(z == end)
+            def _():
+                along(z - d, source, 1).wait_recv()
+
+            @pl.when(z == 0)
+            def _():
+                along(z + d, source, -1).wait_recv()
+
+    def flow(source, d, near):
+        if source >= n_cp:
+            return
+        rights = (z == end - 1) if near else (z < end - 1)
+        lefts = (z == 1) if near else (z > 1)
+
+        @pl.when(inner & rights & (z - d >= 0))
+        def _():
+            if d > 0:
+                along(z - d, source, 1).wait_recv()
+            along(z - d, source, 1).start()
+
+        @pl.when(inner & lefts & (z + d < n_tp))
+        def _():
+            if d > 0:
+                along(z + d, source, -1).wait_recv()
+            along(z + d, source, -1).start()
+
+    def far(source):
+        with jax.named_scope("far"):
+            for d in range(1, end):
+                flow(source, d, False)
+            flow(source + 2, 0, False)
+
+    def near(source):
+        with jax.named_scope("near"):
+            for d in range(1, end):
+                flow(source, d, True)
+            flow(source + 2, 0, True)
+
+    def ends(source):
+        with jax.named_scope("ends"):
+            end_waits(source)
+
+    def project(k):
+        count = sizes[k] * unit
+        x = jnp.concatenate(
+            [rows[o, blocks_of(k)].reshape(count, width) for o in range(n_tp)], axis=1
+        )
+        cos_t, sin_t = cosine[lines_of(k), :], sine[lines_of(k), :]
         raw = dot(x, w[:, q_width:])
         key = turn(raw[:, :HEAD_WIDTH], cos_t, sin_t)
         value = raw[:, HEAD_WIDTH:].astype(jnp.bfloat16)
-        tile = jnp.concatenate([key, value], axis=1).reshape(per, share, 2 * HEAD_WIDTH)
-        kv_own[span] = tile
-        kv_all[span, pl.ds(c, 1)] = tile[:, None]
+        tile = jnp.concatenate([key, value], axis=1)
+        tile = tile.reshape(sizes[k] * per, share, 2 * HEAD_WIDTH)
+        kv_own[blocks_of(k)] = tile
+        kv_all[blocks_of(k), pl.ds(c, 1)] = tile[:, None]
         for i in range(1, n_cp):
-            keys_to(i, t).start()
+            keys_to(i, k).start()
         raw_q = dot(x, w[:, :q_width])
         for h in range(heads):
-            q_all[t, h * count : (h + 1) * count] = turn(
+            q_all[pl.ds(firsts[k] * unit * heads + h * count, count), :] = turn(
                 raw_q[:, h * HEAD_WIDTH : (h + 1) * HEAD_WIDTH], cos_t, sin_t
             )
 
-    def attend(t):
-        lines = pl.ds(pl.multiple_of(t * count, count), count)
-        q = q_all[t]
-        start = jnp.tile(starts[lines, :], (heads, 1))[:, :1]
-        token = jnp.tile(tokens[lines, :], (heads, 1))[:, :1]
-        keys = per * BLOCK
-
-        def more(k, carry):
-            top, total, out = carry
-            u = t - k
-            span = pl.ds(u * per, per)
+    def attend(k):
+        count = sizes[k] * unit
+        q = q_all[pl.ds(firsts[k] * unit * heads, heads * count), :]
+        start = jnp.tile(starts[lines_of(k), :], (heads, 1))[:, :1]
+        token = jnp.tile(tokens[lines_of(k), :], (heads, 1))[:, :1]
+
+        def scored(source, size, diagonal):
+            keys = size * per * BLOCK
+            span = pl.ds(source * per, size * per)
             key = kv_all[span, :, :, :HEAD_WIDTH].reshape(keys, HEAD_WIDTH)
             value = kv_all[span, :, :, HEAD_WIDTH:].reshape(keys, HEAD_WIDTH)
             score = lax.dot_general(
                 q, key, (((1,), (1,)), ((), ())), preferred_element_type=jnp.float32
             )
-            index = u * keys + lax.broadcasted_iota(jnp.int32, score.shape, 1)
-            score = jnp.where((index >= start) & (index <= token), score, masked_score)
+            index = source * (per * BLOCK) + lax.broadcasted_iota(jnp.int32, score.shape, 1)
+            allowed = index >= start
+            if diagonal:
+                allowed = allowed & (index <= token)
+            return jnp.where(allowed, score, masked_score), value
+
+        def lane_sums(weight):
+            partial = weight[:, :HEAD_WIDTH]
+            for g in range(1, weight.shape[1] // HEAD_WIDTH):
+                partial = partial + weight[:, g * HEAD_WIDTH : (g + 1) * HEAD_WIDTH]
+            return partial
+
+        def more(source, size, diagonal, carry):
+            top, total, out = carry
+            score, value = scored(source, size, diagonal)
             new_top = jnp.maximum(top, jnp.max(score, axis=1, keepdims=True))
             weight = jnp.exp2((score - new_top) * factor_of)
             factor = jnp.exp2((top - new_top) * factor_of)
-            total = total * factor + jnp.sum(weight, axis=1, keepdims=True)
+            total = total * factor + lane_sums(weight)
             out = out * factor + dot(weight.astype(jnp.bfloat16), value)
             return new_top, total, out
 
         lengths = (heads * count, 1)
-        initial = (
+        carry = (
             jnp.full(lengths, masked_score, jnp.float32),
-            jnp.zeros(lengths, jnp.float32),
             jnp.zeros((heads * count, HEAD_WIDTH), jnp.float32),
-        )
-        _, total, out = lax.fori_loop(0, t + 1, more, initial)
-        out = (out / total).astype(jnp.bfloat16)
+            jnp.zeros((heads * count, HEAD_WIDTH), jnp.float32),
+        )
+        pairs = firsts[k] // 2
+        if pairs > 0:
+            carry = lax.fori_loop(0, pairs, lambda j, held: more(2 * j, 2, False, held), carry)
+        if firsts[k] % 2:
+            carry = more(firsts[k] - 1, 1, False, carry)
+        with jax.named_scope("kvwait"):
+            arrive(k)
+        carry = more(firsts[k], sizes[k], True, carry)
+        _, total, out = carry
+        out = (out / jnp.sum(total, axis=1, keepdims=True)).astype(jnp.bfloat16)
         return jnp.concatenate([out[h * count : (h + 1) * count] for h in range(heads)], axis=1)
 
-    def output(t, attended):
+    def output(k, attended):
         high = z // (n_tp // 2)
-        for k in range(n_tp):
-            o = (1 - high) * (end - k) + high * k
+        for turn_of in range(n_tp):
+            o = (1 - high) * (end - turn_of) + high * turn_of
             product = dot(attended, wo[o])
             go_right = (z == 0) & (o > z)
             go_left = (z == end) & (o < z)
 
             @pl.when(go_right)
             def _():
-                to_right[o, t] = product.astype(jnp.bfloat16)
-                rightward(o, t).start()
+                to_right[o, lines_of(k)] = product.astype(jnp.bfloat16)
+                rightward(o, k).start()
 
             @pl.when(go_left)
             def _():
-                to_left[o, t] = product.astype(jnp.bfloat16)
-                leftward(o, t).start()
+                to_left[o, lines_of(k)] = product.astype(jnp.bfloat16)
+                leftward(o, k).start()
 
             @pl.when(jnp.logical_not(go_right | go_left))
             def _():
-                part[o, t] = product
-
-    def reduce(s):
-        t_right = s - 1 - z
-        t_left = s - 1 - (end - z)
-
-        @pl.when((z > 0) & (t_right >= 0) & (t_right < n_cp))
-        def _():
-            for o in range(end, 0, -1):
-                @pl.when(o > z)
-                def _():
-                    rightward(o, t_right).wait_recv()
-                    total = part[o, t_right] + from_left[o, t_right].astype(jnp.float32)
-                    to_right[o, t_right] = total.astype(jnp.bfloat16)
-                    rightward(o, t_right).start()
-
-        @pl.when((z < end) & (t_left >= 0) & (t_left < n_cp))
-        def _():
-            for o in range(end):
-                @pl.when(o < z)
-                def _():
-                    leftward(o, t_left).wait_recv()
-                    total = part[o, t_left] + from_right[o, t_left].astype(jnp.float32)
-                    to_left[o, t_left] = total.astype(jnp.bfloat16)
-                    leftward(o, t_left).start()
-
-    def finish(t):
+                part[o, lines_of(k)] = product
+
+    def hop(k, h):
+        lines = lines_of(k)
+
+        @pl.when(z == h)
+        def _():
+            for o in range(end, h, -1):
+                rightward(o, k).wait_recv()
+                total = part[o, lines] + from_left[o, lines].astype(jnp.float32)
+                to_right[o, lines] = total.astype(jnp.bfloat16)
+                rightward(o, k).start()
+
+        @pl.when(z == end - h)
+        def _():
+            for o in range(end - h):
+                leftward(o, k).wait_recv()
+                total = part[o, lines] + from_right[o, lines].astype(jnp.float32)
+                to_left[o, lines] = total.astype(jnp.bfloat16)
+                leftward(o, k).start()
+
+    def finish(k):
+        lines = lines_of(k)
+
         @pl.when(z > 0)
         def _():
-            rightward(z, t).wait_recv()
-            part[z, t] += from_left[z, t].astype(jnp.float32)
+            rightward(z, k).wait_recv()
+            part[z, lines] += from_left[z, lines].astype(jnp.float32)
 
         @pl.when(z < end)
         def _():
-            leftward(z, t).wait_recv()
-            part[z, t] += from_right[z, t].astype(jnp.float32)
-
-        done[pl.ds(t * per, per)] = part[z, t].astype(jnp.bfloat16).reshape(per, share, width)
-
-    @pl.loop(0, n_cp + 2 * n_tp - 1)
-    def _(step):
-        s = step - end
-        gather(s)
-        reduce(s)
-
-        @pl.when((s >= 0) & (s < n_cp))
-        def _():
-            @pl.when(s == 0)
-            def _():
-                for copy in weights:
-                    copy.wait()
-
-            project(s)
-
-        @pl.when((s >= 1) & (s <= n_cp))
-        def _():
-            @pl.when(s == 1)
-            def _():
-                for o in range(n_tp):
-                    out_weight(o).wait()
-
-            for i in range(1, n_cp):
-                keys_to(i, s - 1).wait_recv()
-            output(s - 1, attend(s - 1))
-
-        @pl.when(s >= n_tp)
-        def _():
-            finish(s - n_tp)
-
-    for b in range(blocks):
-        rank = jnp.int32(0)
-        for e in range(b):
-            rank += (owner[e] == owner[b]).astype(jnp.int32)
-        order[b] = owner[b] * per + rank
-    for b in range(blocks):
-        def seek(e, found):
-            return jnp.where(order[e] == b, e, found)
-        source = lax.fori_loop(0, blocks, seek, jnp.int32(0))
-        outgoing[b] = done[source]
-    for i in range(1, n_cp):
-        final(i).start()
-    out_ref[:, pl.ds(c, 1)] = outgoing[pl.ds(c * per, per)][:, None]
-    for i in range(1, n_cp):
-        final(i).wait_recv()
-        source = lax.rem(c - i + n_cp, n_cp)
-        out_ref[:, pl.ds(source, 1)] = landed[:, pl.ds(source, 1)]
-    for i in range(1, n_cp):
-        spread(i).wait_send()
-        final(i).wait_send()
-
-    @pl.loop(0, n_cp)
-    def _(t):
+            leftward(z, k).wait_recv()
+            part[z, lines] += from_right[z, lines].astype(jnp.float32)
+
+        summed = part[z, lines].astype(jnp.bfloat16)
+        done[blocks_of(k)] = summed.reshape(sizes[k] * per, share, width)
+
+    def arrive(k):
+        landed_keys = kv_all.at[blocks_of(k), pl.ds(0, n_cp - 1)]
+        pltpu.make_async_copy(landed_keys, landed_keys, k_recv.at[k]).wait()
+
+    def reduce(k, h):
+        with jax.named_scope("reduce"):
+            hop(k, h)
+
+    with jax.named_scope("fill"):
+        for source in range(n_cp):
+            take(source)
+            if source == 0:
+                first_sends()
+                continue
+            end_sends(source)
+            if source <= 2:
+                flow(source, 0, False)
+                flow(source, 0, True)
+        first_waits()
+    pltpu.make_async_copy(w, w, w_sem).wait()
+    passed, reached = 0, 0
+
+    def pass_on(fars, nears):
+        nonlocal passed, reached
+        while passed < min(fars, n_cp - 1):
+            passed += 1
+            far(passed)
+        while reached < min(nears, n_cp - 1):
+            reached += 1
+            near(reached)
+
+    for k in range(last):
+        pass_on(2 * firsts[k] + 2 * sizes[k] - 2, firsts[k + 1] - 1)
+        for source in range(max(firsts[k], 1), firsts[k + 1]):
+            ends(source)
+        with jax.named_scope("project"):
+            project(k)
+        if k == 0:
+            pass_on(2, 0)
+            pltpu.make_async_copy(wo, wo, o_sem).wait()
+        else:
+            pass_on(n_cp if k > 1 else 5, firsts[k + 1])
+        if k == last - 1:
+            for e in range(last - 2):
+                reduce(e, end - 1)
+        with jax.named_scope("attend"):
+            attended = attend(k)
+        pass_on(n_cp if k > 0 else 3, firsts[k + 1] + (1 if k > 0 else 0))
+        with jax.named_scope("output"):
+            output(k, attended)
+        if k > 0 and k < last - 1:
+            for h in range(1, end - 1):
+                if k - h >= 0:
+                    reduce(k - h, h)
+    with jax.named_scope("finish"):
+        for k in range(last - 2):
+            finish(k)
+    for k in range(max(last - 2, 0), last):
+        for h in range(1, end):
+            reduce(k, h)
+    with jax.named_scope("finish"):
+        for k in range(max(last - 2, 0), last):
+            finish(k)
+
+    with jax.named_scope("a2a"):
+        for b in range(blocks):
+            outgoing[b] = done[order[b]]
         for i in range(1, n_cp):
-            keys_to(i, t).wait_send()
-        for o in range(n_tp):
-            @pl.when((z < end) & (o <= z))
-            def _():
-                along(o, t, 1).wait_send()
-
-            @pl.when((z > 0) & (o >= z))
-            def _():
-                along(o, t, -1).wait_send()
-
-            @pl.when(o > z)
-            def _():
-                rightward(o, t).wait_send()
-
-            @pl.when(o < z)
-            def _():
-                leftward(o, t).wait_send()
+            final(i).start()
+        out_ref[:, pl.ds(c, 1)] = outgoing[pl.ds(c * per, per)][:, None]
+        others = landed.at[:, pl.ds(0, n_cp - 1)]
+        pltpu.make_async_copy(others, others, a_recv).wait()
+        for i in range(1, n_cp):
+            source = lax.rem(c - i + n_cp, n_cp)
+            out_ref[:, pl.ds(source, 1)] = landed[:, pl.ds(source, 1)]
+
+    def drain(ref, sem):
+        pltpu.make_async_copy(ref, ref, sem).wait()
+
+    drain(landed.at[:, pl.ds(0, n_cp - 1)], s_send)
+    drain(landed.at[:, pl.ds(0, n_cp - 1)], a_send)
+    drain(kv_all.at[:, pl.ds(0, n_cp - 1)], k_send)
+    for step in (1, -1):
+        @pl.when((z + 2 * step >= 0) & (z + 2 * step < n_tp))
+        def _():
+            skip(step).wait_send()
+
+    for v in range(n_tp):
+        @pl.when(z == v)
+        def _():
+            if v < end:
+                pieces = (n_cp - 1) * (v + 1) + max(v, 1)
+                drain(wo.at[0, pl.ds(0, pieces * unit)], r_send)
+                drain(to_right.at[pl.ds(0, end - v)], pr_send)
+            if v > 0:
+                pieces = (n_cp - 1) * (n_tp - v) + max(end - v, 1)
+                drain(wo.at[0, pl.ds(0, pieces * unit)], l_send)
+                drain(to_left.at[pl.ds(0, v)], pl_send)
 
 
 def fused_call(bounds, owner, hidden, wq, wk, wv, wo, inverse, n_cp, n_tp):
     rows, width = hidden.shape
     per = rows // BLOCK
     share = BLOCK // n_cp
-    blocks, count = per * n_cp, per * share
+    blocks = per * n_cp
     heads = wq.shape[1] // HEAD_WIDTH
+    sizes = chunk_sizes(n_cp)
     pieces = hidden.reshape(per, n_cp, share, width)
     bf, f32, i32, dma = jnp.bfloat16, jnp.float32, jnp.int32, pltpu.SemaphoreType.DMA
     vmem = pl.BlockSpec(memory_space=pltpu.VMEM)
     hbm = pl.BlockSpec(memory_space=pltpu.HBM)
     smem = pl.BlockSpec(memory_space=pltpu.SMEM)
-    slab = (n_tp, n_cp, count, width)
+    slab = (n_tp, rows, width)
     kv_width = 2 * HEAD_WIDTH
-    sems = dma((n_tp, n_cp))
+    sums = dma((n_tp - 1, len(sizes)))
     flops = 2 * rows * (wq.shape[0] * (wq.shape[1] + kv_width) + wo.shape[0] * wo.shape[1])
     out = pl.pallas_call(
-        functools.partial(fused_kernel, n_cp, n_tp),
+        functools.partial(fused_kernel, n_cp, n_tp, sizes),
         out_shape=jax.ShapeDtypeStruct((per, n_cp, share, width), bf),
         in_specs=[smem, smem, hbm, hbm, hbm, hbm, hbm, vmem],
         out_specs=vmem,
@@ -548,7 +669,7 @@
             pltpu.VMEM((n_tp, wo.shape[0], width), bf),
             pltpu.VMEM((rows, HEAD_WIDTH), f32), pltpu.VMEM((rows, HEAD_WIDTH), f32),
             pltpu.VMEM((rows, HEAD_WIDTH), i32), pltpu.VMEM((rows, HEAD_WIDTH), i32),
-            pltpu.VMEM((n_cp, heads * count, HEAD_WIDTH), bf),
+            pltpu.VMEM((rows * heads, HEAD_WIDTH), bf),
             pltpu.VMEM((blocks, share, kv_width), bf),
             pltpu.VMEM((blocks, n_cp, share, kv_width), bf),
             pltpu.VMEM(slab, f32),
@@ -557,9 +678,8 @@
             pltpu.VMEM((blocks, share, width), bf),
             pltpu.VMEM((per, n_cp, share, width), bf),
             pltpu.SMEM((blocks,), i32),
-            dma((3,)), dma((n_tp,)), dma, dma((n_cp,)), dma((n_cp,)), sems, sems, sems,
-            dma((n_cp, n_cp)), dma((n_cp, n_cp)),
-            sems, sems, sems, sems, dma((n_cp,)), dma((n_cp,)),
+            dma, dma, dma, dma, dma((n_cp,)), dma((2,)), dma, dma, dma((n_tp, n_cp)),
+            dma, dma((len(sizes),)), dma, dma, sums, sums, dma, dma,
         ],
         compiler_params=pltpu.CompilerParams(
             collective_id=1, has_side_effects=True, vmem_limit_bytes=VMEM_LIMIT

time: 103 us -> 85.5 us (0.83)
  Pallas kernels: 100 us -> 83.1 us
    pallas_call x1, Pallas kernels: 100 us -> 83.1 us  [fused_call(): pl.pallas_call(functools.partial(fused_kernel, n_cp, n_tp, sizes), out_sh...]
    unnamed x1 -> x5, local copies, waits for them, and re-layouts: 1.87 us -> 2.11 us
where the time goes in v2:
time: 85.5 us; the launch traced here: 85.3 us
  Pallas kernels  83.1 us (97%)
  local copies, waits for them, and re-layouts  2.2 us (3%)
    pallas_call x1, Pallas kernels, fused_call(): pl.pallas_call(functools.partial(fused_kernel, n_cp, n_tp, sizes), out_sh...  83.1 us
    unnamed x5, local copies, waits for them, and re-layouts  2.11 us

profile of v2, /device:TPU:1, one launch (start us, length us, event | category | flops | bytes accessed | tf_op | source)
XLA Modules:
  0.0 85.3 jit_solution(8194484751562372284)
XLA Ops:
  0.0 0.1 broadcast_in_dim_tile.3.inverse
  0.1 0.0 copy-start
  0.1 0.7 copy-done
  0.8 0.0 copy-start.1
  0.8 0.7 copy-done.1
  1.4 83.1 %shard_map.73 = bf16[2,8,16,1024]{3,2,1,0:T(8,128)(2,1)S(1)} custom-call(s32[9]{0:T(128)S(1)} %copy-done, s32[16]{0:T(128)S(1)} %copy-done.1, bf16[2,8,16,1024]{3,2,1,0:T(8,128)(2,1)} %bitcast.3, bf16[4096,1024]{1,0:T(8,128)(2,1)} %wq_hbm.1, bf16[4096,128]{1,0:T(8,128)(2,1)} %wk_hbm.1, bf16[4096,128]{1,0:T(8,128)(2,1)} %wv_hbm.1, bf16[1024,4096]{1,0:T(8,128)(2,1)} %wo_hbm.1, ...), custom_call_target="tpu_custom_call" | custom-call | flops 4831838208 | bytes 20971520 | tf_op jit(solution)/shard_map/pallas_call | solution.py:661
  84.5 0.8 copy.9
  (2 shorter events, 0.0 us)
Async XLA Ops:
  0.1 0.7 copy-start
  0.8 0.7 copy-start.1

commit v3 on v2

--- a/solution.py
+++ b/solution.py
@@ -166,10 +166,17 @@
 
 MESH = pl.DeviceIdType.MESH
 VMEM_LIMIT = 53 << 20
+PASS_ROWS = 128
+LEAD = 3
 
 
 def dot(a, b):
     return jnp.dot(a, b, preferred_element_type=jnp.float32)
+
+
+def fill_rows(x):
+    copies = max(PASS_ROWS // x.shape[0], 1)
+    return jnp.concatenate([x] * copies, axis=0) if copies > 1 else x
 
 
 def turn(raw, cosine, sine):
@@ -197,7 +204,7 @@
         + lax.broadcasted_iota(jnp.int32, shape, 1) + offset
     )
     start = jnp.zeros_like(token)
-    for i in range(bounds.shape[0] - 1):
+    for i in range(len(bounds) - 1):
         start = jnp.where(token >= bounds[i], bounds[i], start)
     return token, start
 
@@ -205,19 +212,21 @@
 def chunk_sizes(sources):
     if sources < 4 or sources % 2:
         return [1] * sources
-    return [1] + [2] * ((sources - 2) // 2) + [1]
+    return [2] * ((sources - 2) // 2) + [1, 1]
 
 
 def fused_kernel(
-    n_cp, n_tp, sizes,
-    bounds, owner, hidden, wq_hbm, wk_hbm, wv_hbm, wo_hbm, inverse,
+    n_cp, n_tp, sizes, bound_count,
+    table, hidden, wq_hbm, wk_hbm, wv_hbm, wo_hbm, inverse,
     out_ref,
     rows, w, wo, cosine, sine, tokens, starts, q_all, kv_own, kv_all,
     part, from_left, from_right, to_right, to_left, done, outgoing, landed, order,
-    w_sem, o_sem, own_sem, s_send, s_recv, d_send, r_send, l_send, z_recv, k_send, k_recv,
+    w_sem, o_sem, own_sem, s_send, s_recv, r_send, l_send, z_recv, k_send, k_recv,
     pr_send, pl_send, pr_recv, pl_recv, a_send, a_recv,
 ):
     c, z = lax.axis_index("cp"), lax.axis_index("tp")
+    bounds = [table[i] for i in range(bound_count)]
+    owner = [table[bound_count + b] for b in range(table.shape[0] - bound_count)]
     per, share, width = hidden.shape[0], hidden.shape[2], hidden.shape[3]
     blocks = per * n_cp
     unit = per * share
@@ -257,14 +266,6 @@
             src_ref=piece, dst_ref=piece,
             send_sem=sems, recv_sem=z_recv.at[origin, source],
             device_id={"tp": lax.rem(z + step + n_tp, n_tp)}, device_id_type=MESH,
-        )
-
-    def skip(step):
-        piece = rows.at[z, pl.ds(0, per)]
-        return pltpu.make_async_remote_copy(
-            src_ref=piece, dst_ref=piece,
-            send_sem=d_send.at[(step + 1) // 2], recv_sem=z_recv.at[z, 0],
-            device_id={"tp": lax.rem(z + 2 * step + n_tp, n_tp)}, device_id_type=MESH,
         )
 
     def blocks_of(k):
@@ -345,27 +346,6 @@
         def _():
             along(z, source, -1).start()
 
-    def first_sends():
-        for step in (1, -1):
-            @pl.when((z + step >= 0) & (z + step < n_tp))
-            def _():
-                along(z, 0, step).start()
-
-            @pl.when((z + 2 * step >= 0) & (z + 2 * step < n_tp))
-            def _():
-                skip(step).start()
-
-    def first_waits():
-        for d in range(1, n_tp):
-            for step in (1, -1):
-                @pl.when((z - step * d >= 0) & (z - step * d < n_tp))
-                def _():
-                    along(z - step * d, 0, step).wait_recv()
-                    if d > 1:
-                        @pl.when((z + step >= 0) & (z + step < n_tp))
-                        def _():
-                            along(z - step * d, 0, step).start()
-
     def end_waits(source):
         for d in range(1, n_tp):
             @pl.when(z == end)
@@ -398,7 +378,7 @@
         with jax.named_scope("far"):
             for d in range(1, end):
                 flow(source, d, False)
-            flow(source + 2, 0, False)
+            flow(source + 1, 0, False)
 
     def near(source):
         with jax.named_scope("near"):
@@ -416,7 +396,8 @@
             [rows[o, blocks_of(k)].reshape(count, width) for o in range(n_tp)], axis=1
         )
         cos_t, sin_t = cosine[lines_of(k), :], sine[lines_of(k), :]
-        raw = dot(x, w[:, q_width:])
+        x = fill_rows(x)
+        raw = dot(x, w[:, q_width:])[:count]
         key = turn(raw[:, :HEAD_WIDTH], cos_t, sin_t)
         value = raw[:, HEAD_WIDTH:].astype(jnp.bfloat16)
         tile = jnp.concatenate([key, value], axis=1)
@@ -425,7 +406,7 @@
         kv_all[blocks_of(k), pl.ds(c, 1)] = tile[:, None]
         for i in range(1, n_cp):
             keys_to(i, k).start()
-        raw_q = dot(x, w[:, :q_width])
+        raw_q = dot(x, w[:, :q_width])[:count]
         for h in range(heads):
             q_all[pl.ds(firsts[k] * unit * heads + h * count, count), :] = turn(
                 raw_q[:, h * HEAD_WIDTH : (h + 1) * HEAD_WIDTH], cos_t, sin_t
@@ -487,32 +468,49 @@
 
     def output(k, attended):
         high = z // (n_tp // 2)
+        count = attended.shape[0]
+        attended = fill_rows(attended)
         for turn_of in range(n_tp):
             o = (1 - high) * (end - turn_of) + high * turn_of
-            product = dot(attended, wo[o])
+            product = dot(attended, wo[o])[:count]
             go_right = (z == 0) & (o > z)
             go_left = (z == end) & (o < z)
 
             @pl.when(go_right)
             def _():
                 to_right[o, lines_of(k)] = product.astype(jnp.bfloat16)
-                rightward(o, k).start()
 
             @pl.when(go_left)
             def _():
                 to_left[o, lines_of(k)] = product.astype(jnp.bfloat16)
+
+            @pl.when(go_right & (o > z + 1))
+            def _():
+                rightward(o, k).start()
+
+            @pl.when(go_left & (o < z - 1))
+            def _():
                 leftward(o, k).start()
 
             @pl.when(jnp.logical_not(go_right | go_left))
             def _():
                 part[o, lines_of(k)] = product
 
-    def hop(k, h):
+    def adjacent(k):
+        @pl.when(z == 0)
+        def _():
+            rightward(1, k).start()
+
+        @pl.when(z == end)
+        def _():
+            leftward(end - 1, k).start()
+
+    def hop(k, h, dests):
         lines = lines_of(k)
 
         @pl.when(z == h)
         def _():
-            for o in range(end, h, -1):
+            for o in list(range(end, h, -1))[dests]:
                 rightward(o, k).wait_recv()
                 total = part[o, lines] + from_left[o, lines].astype(jnp.float32)
                 to_right[o, lines] = total.astype(jnp.bfloat16)
@@ -520,7 +518,7 @@
 
         @pl.when(z == end - h)
         def _():
-            for o in range(end - h):
+            for o in list(range(end - h))[dests]:
                 leftward(o, k).wait_recv()
                 total = part[o, lines] + from_right[o, lines].astype(jnp.float32)
                 to_left[o, lines] = total.astype(jnp.bfloat16)
@@ -546,23 +544,38 @@
         landed_keys = kv_all.at[blocks_of(k), pl.ds(0, n_cp - 1)]
         pltpu.make_async_copy(landed_keys, landed_keys, k_recv.at[k]).wait()
 
-    def reduce(k, h):
-        with jax.named_scope("reduce"):
-            hop(k, h)
+    def reduce(k, h, dests=slice(None)):
+        with jax.named_scope(f"reduce{k}{h}"):
+            hop(k, h, dests)
 
     with jax.named_scope("fill"):
         for source in range(n_cp):
             take(source)
+            end_sends(source)
+            if source < 2:
+                flow(source, 0, False)
+            if source < LEAD:
+                flow(source, 0, True)
+        for source in range(LEAD):
+            for d in range(1, end):
+                flow(source, d, False)
             if source == 0:
-                first_sends()
-                continue
-            end_sends(source)
-            if source <= 2:
-                flow(source, 0, False)
-                flow(source, 0, True)
-        first_waits()
+                flow(2, 0, False)
+            if source == LEAD - 1:
+                for d in range(2, end):
+                    flow(0, d, True)
+            if end > 1:
+                flow(source, 1, True)
+        for source in range(1, LEAD):
+            for d in range(2, end):
+                flow(source, d, True)
+        flow(LEAD, 0, True)
+        flow(LEAD, 0, False)
+        far(LEAD)
+        flow(LEAD + 1, 0, True)
+        ends(0)
     pltpu.make_async_copy(w, w, w_sem).wait()
-    passed, reached = 0, 0
+    passed, reached = LEAD, LEAD - 1
 
     def pass_on(fars, nears):
         nonlocal passed, reached
@@ -573,37 +586,58 @@
             reached += 1
             near(reached)
 
-    for k in range(last):
-        pass_on(2 * firsts[k] + 2 * sizes[k] - 2, firsts[k + 1] - 1)
+    parts = (slice(0, 1), slice(1, None))
+    hops = [(k, h, p) for k in range(last) for h in range(1, end) for p in range(2)]
+    held = {}
+
+    def run(k, h, *wanted):
+        for p in wanted:
+            if (k, h, p) in hops:
+                hops.remove((k, h, p))
+                reduce(k, h, parts[p])
+
+    def projection(k):
+        pass_on(0, firsts[k + 1] - 1)
         for source in range(max(firsts[k], 1), firsts[k + 1]):
             ends(source)
         with jax.named_scope("project"):
             project(k)
-        if k == 0:
-            pass_on(2, 0)
-            pltpu.make_async_copy(wo, wo, o_sem).wait()
-        else:
-            pass_on(n_cp if k > 1 else 5, firsts[k + 1])
-        if k == last - 1:
-            for e in range(last - 2):
-                reduce(e, end - 1)
+
+    def attention(k):
         with jax.named_scope("attend"):
-            attended = attend(k)
-        pass_on(n_cp if k > 0 else 3, firsts[k + 1] + (1 if k > 0 else 0))
+            held[k] = attend(k)
+
+    def result(k):
         with jax.named_scope("output"):
-            output(k, attended)
-        if k > 0 and k < last - 1:
-            for h in range(1, end - 1):
-                if k - h >= 0:
-                    reduce(k - h, h)
+            output(k, held.pop(k))
+
+    def adjacents(*chosen):
+        for k in chosen:
+            adjacent(k)
+
+    if last == 5:
+        plan = [
+            (projection, 0), (pass_on, 5, 3), (attention, 0), (pass_on, 6, 4),
+            (result, 0), (adjacents, 0),
+            (projection, 1), (pass_on, n_cp, 6), (attention, 1), (pass_on, n_cp, n_cp),
+            (result, 1), (adjacents, 1), (run, 0, 1, 0, 1),
+            (projection, 2), (projection, 3), (attention, 2), (run, 1, 1, 0),
+            (result, 2), (run, 1, 1, 1), (run, 0, 2, 0, 1),
+            (projection, 4), (attention, 3), (run, 2, 1, 0), (result, 3), (run, 2, 1, 1),
+            (run, 1, 2, 0, 1), (attention, 4), (run, 3, 1, 0), (result, 4), (adjacents, 2, 3, 4),
+            (run, 3, 1, 1), (run, 2, 2, 0, 1), (run, 4, 1, 0), (run, 3, 2, 0, 1),
+        ]
+    else:
+        plan = []
+        for k in range(last):
+            plan += [(projection, k), (pass_on, n_cp, n_cp), (attention, k), (result, k), (adjacents, k)]
+    pltpu.make_async_copy(wo, wo, o_sem).wait()
+    for step, *given in plan:
+        step(*given)
+    for k, h, p in list(hops):
+        reduce(k, h, parts[p])
     with jax.named_scope("finish"):
-        for k in range(last - 2):
-            finish(k)
-    for k in range(max(last - 2, 0), last):
-        for h in range(1, end):
-            reduce(k, h)
-    with jax.named_scope("finish"):
-        for k in range(max(last - 2, 0), last):
+        for k in range(last):
             finish(k)
 
     with jax.named_scope("a2a"):
@@ -624,21 +658,14 @@
     drain(landed.at[:, pl.ds(0, n_cp - 1)], s_send)
     drain(landed.at[:, pl.ds(0, n_cp - 1)], a_send)
     drain(kv_all.at[:, pl.ds(0, n_cp - 1)], k_send)
-    for step in (1, -1):
-        @pl.when((z + 2 * step >= 0) & (z + 2 * step < n_tp))
-        def _():
-            skip(step).wait_send()
-
     for v in range(n_tp):
         @pl.when(z == v)
         def _():
             if v < end:
-                pieces = (n_cp - 1) * (v + 1) + max(v, 1)
-                drain(wo.at[0, pl.ds(0, pieces * unit)], r_send)
+                drain(rows.at[pl.ds(0, v + 1)], r_send)
                 drain(to_right.at[pl.ds(0, end - v)], pr_send)
             if v > 0:
-                pieces = (n_cp - 1) * (n_tp - v) + max(end - v, 1)
-                drain(wo.at[0, pl.ds(0, pieces * unit)], l_send)
+                drain(rows.at[pl.ds(0, n_tp - v)], l_send)
                 drain(to_left.at[pl.ds(0, v)], pl_send)
 
 
@@ -659,9 +686,9 @@
     sums = dma((n_tp - 1, len(sizes)))
     flops = 2 * rows * (wq.shape[0] * (wq.shape[1] + kv_width) + wo.shape[0] * wo.shape[1])
     out = pl.pallas_call(
-        functools.partial(fused_kernel, n_cp, n_tp, sizes),
+        functools.partial(fused_kernel, n_cp, n_tp, sizes, bounds.shape[0]),
         out_shape=jax.ShapeDtypeStruct((per, n_cp, share, width), bf),
-        in_specs=[smem, smem, hbm, hbm, hbm, hbm, hbm, vmem],
+        in_specs=[smem, hbm, hbm, hbm, hbm, hbm, vmem],
         out_specs=vmem,
         scratch_shapes=[
             pltpu.VMEM((n_tp, blocks, share, width), bf),
@@ -678,14 +705,14 @@
             pltpu.VMEM((blocks, share, width), bf),
             pltpu.VMEM((per, n_cp, share, width), bf),
             pltpu.SMEM((blocks,), i32),
-            dma, dma, dma, dma, dma((n_cp,)), dma((2,)), dma, dma, dma((n_tp, n_cp)),
+            dma, dma, dma, dma, dma((n_cp,)), dma, dma, dma((n_tp, n_cp)),
             dma, dma((len(sizes),)), dma, dma, sums, sums, dma, dma,
         ],
         compiler_params=pltpu.CompilerParams(
             collective_id=1, has_side_effects=True, vmem_limit_bytes=VMEM_LIMIT
         ),
         cost_estimate=pl.CostEstimate(flops=flops, bytes_accessed=20 << 20, transcendentals=0),
-    )(bounds, owner, pieces, wq, wk, wv, wo, inverse)
+    )(jnp.concatenate([bounds, owner]), pieces, wq, wk, wv, wo, inverse)
     return out.reshape(rows, width)
 
 

time: 85.5 us -> 80.2 us (0.938)
  Pallas kernels: 83.1 us -> 77.9 us
  local copies, waits for them, and re-layouts: 2.2 us -> 0.88 us
    pallas_call x1, Pallas kernels: 83.1 us -> 77.9 us  [fused_call(): pl.pallas_call(functools.partial(fused_kernel, n_cp, n_tp, sizes, bounds....]
    unnamed x5 -> x1, local copies, waits for them, and re-layouts: 2.11 us -> 0.8 us
where the time goes in v3:
time: 80.2 us; the launch traced here: 79.5 us
  Pallas kernels  77.9 us (97%)
  local copies, waits for them, and re-layouts  0.88 us (1%)
    pallas_call x1, Pallas kernels, fused_call(): pl.pallas_call(functools.partial(fused_kernel, n_cp, n_tp, sizes, bounds....  77.9 us

profile of v3, /device:TPU:1, one launch (start us, length us, event | category | flops | bytes accessed | tf_op | source)
XLA Modules:
  0.0 79.5 jit_solution(9470264304152906583)
XLA Ops:
  0.0 0.7 pad_add_fusion.table
  0.8 0.1 broadcast_in_dim_tile.3.inverse
  0.9 77.9 %shard_map.73 = bf16[2,8,16,1024]{3,2,1,0:T(8,128)(2,1)S(1)} custom-call(s32[25]{0:T(128)S(1)} %pad_add_fusion.table, bf16[2,8,16,1024]{3,2,1,0:T(8,128)(2,1)} %bitcast.3, bf16[4096,1024]{1,0:T(8,128)(2,1)} %wq_hbm.1, bf16[4096,128]{1,0:T(8,128)(2,1)} %wk_hbm.1, bf16[4096,128]{1,0:T(8,128)(2,1)} %wv_hbm.1, bf16[1024,4096]{1,0:T(8,128)(2,1)} %wo_hbm.1, ...), custom_call_target="tpu_custom_call" | custom-call | flops 4831838208 | bytes 20971520 | tf_op jit(solution)/shard_map/pallas_call | solution.py:688
  78.7 0.8 %copy.9 = bf16[256,1024]{1,0:T(8,128)(2,1)} copy(bf16[256,1024]{1,0:T(8,128)(2,1)S(1)} %bitcast.2) | data formatting | bytes 1048576
  (2 shorter events, 0.0 us)

commit v4 on v3

--- a/solution.py
+++ b/solution.py
@@ -212,16 +212,16 @@
 def chunk_sizes(sources):
     if sources < 4 or sources % 2:
         return [1] * sources
-    return [2] * ((sources - 2) // 2) + [1, 1]
+    return [2] * (sources // 2)
 
 
 def fused_kernel(
     n_cp, n_tp, sizes, bound_count,
     table, hidden, wq_hbm, wk_hbm, wv_hbm, wo_hbm, inverse,
     out_ref,
-    rows, w, wo, cosine, sine, tokens, starts, q_all, kv_own, kv_all,
+    mine, rows, w, wo, cosine, sine, tokens, starts, q_all, kv_own, kv_all,
     part, from_left, from_right, to_right, to_left, done, outgoing, landed, order,
-    w_sem, o_sem, own_sem, s_send, s_recv, r_send, l_send, z_recv, k_send, k_recv,
+    w_sem, o_sem, own_sem, m_sem, s_send, s_recv, r_send, l_send, z_recv, k_send, k_recv,
     pr_send, pl_send, pr_recv, pl_recv, a_send, a_recv,
 ):
     c, z = lax.axis_index("cp"), lax.axis_index("tp")
@@ -235,6 +235,10 @@
     end = n_tp - 1
     last = len(sizes)
     firsts = [sum(sizes[:k]) for k in range(last + 1)]
+    spans = [(firsts[k] * unit, sizes[k] * unit) for k in range(last - 1)]
+    spans += [(firsts[last - 1] * unit + b * share, share) for b in range(sizes[-1] * per)]
+    units_of = [[k] for k in range(last - 1)] + [list(range(last - 1, len(spans)))]
+    groups = [[(a, 1) for a in range(firsts[k], firsts[k + 1])] for k in range(last)]
     factor_of = math.log2(math.e) / math.sqrt(HEAD_WIDTH)
     weights = (
         pltpu.make_async_copy(wk_hbm, w.at[:, pl.ds(q_width, HEAD_WIDTH)], w_sem),
@@ -248,13 +252,16 @@
         )
 
     own = pltpu.make_async_copy(hidden.at[:, c], rows.at[z, pl.ds(c * per, per)], own_sem)
+    staged = pltpu.make_async_copy(hidden, mine, m_sem)
+    staged.start()
     own.start()
     greet(n_cp, n_tp)
+    staged.wait()
 
     def spread(i):
         peer = lax.rem(c + i, n_cp)
         return pltpu.make_async_remote_copy(
-            src_ref=hidden.at[:, peer], dst_ref=rows.at[z, pl.ds(c * per, per)],
+            src_ref=mine.at[:, peer], dst_ref=rows.at[z, pl.ds(c * per, per)],
             send_sem=s_send, recv_sem=s_recv.at[i],
             device_id={"cp": peer}, device_id_type=MESH,
         )
@@ -274,24 +281,27 @@
     def lines_of(k):
         return pl.ds(firsts[k] * unit, sizes[k] * unit)
 
-    def keys_to(i, k):
+    def keys_to(i, group):
+        span = pl.ds(group[0] * per, group[1] * per)
         return pltpu.make_async_remote_copy(
-            src_ref=kv_own.at[blocks_of(k)], dst_ref=kv_all.at[blocks_of(k), c],
-            send_sem=k_send, recv_sem=k_recv.at[k],
+            src_ref=kv_own.at[span], dst_ref=kv_all.at[span, c],
+            send_sem=k_send, recv_sem=k_recv.at[group[0]],
             device_id={"cp": lax.rem(c + i, n_cp)}, device_id_type=MESH,
         )
 
-    def rightward(o, k):
+    def rightward(o, u):
+        lines = pl.ds(*spans[u])
         return pltpu.make_async_remote_copy(
-            src_ref=to_right.at[o, lines_of(k)], dst_ref=from_left.at[o, lines_of(k)],
-            send_sem=pr_send, recv_sem=pr_recv.at[o - 1, k],
+            src_ref=to_right.at[o, lines], dst_ref=from_left.at[o, lines],
+            send_sem=pr_send, recv_sem=pr_recv.at[o - 1, u],
             device_id={"tp": lax.rem(z + 1, n_tp)}, device_id_type=MESH,
         )
 
-    def leftward(o, k):
+    def leftward(o, u):
+        lines = pl.ds(*spans[u])
         return pltpu.make_async_remote_copy(
-            src_ref=to_left.at[o, lines_of(k)], dst_ref=from_right.at[o, lines_of(k)],
-            send_sem=pl_send, recv_sem=pl_recv.at[o, k],
+            src_ref=to_left.at[o, lines], dst_ref=from_right.at[o, lines],
+            send_sem=pl_send, recv_sem=pl_recv.at[o, u],
             device_id={"tp": lax.rem(z + n_tp - 1, n_tp)}, device_id_type=MESH,
         )
 
@@ -384,28 +394,37 @@
         with jax.named_scope("near"):
             for d in range(1, end):
                 flow(source, d, True)
-            flow(source + 2, 0, True)
+            if source >= LEAD:
+                flow(source + 1, 0, True)
 
     def ends(source):
         with jax.named_scope("ends"):
             end_waits(source)
 
-    def project(k):
-        count = sizes[k] * unit
-        x = jnp.concatenate(
-            [rows[o, blocks_of(k)].reshape(count, width) for o in range(n_tp)], axis=1
-        )
-        cos_t, sin_t = cosine[lines_of(k), :], sine[lines_of(k), :]
-        x = fill_rows(x)
+    def gathered(first, size):
+        span = pl.ds(first * per, size * per)
+        count = size * unit
+        x = [rows[o, span].reshape(count, width) for o in range(n_tp)]
+        lines = pl.ds(first * unit, count)
+        return fill_rows(jnp.concatenate(x, axis=1)), cosine[lines, :], sine[lines, :]
+
+    def project_keys(group):
+        count = group[1] * unit
+        span = pl.ds(group[0] * per, group[1] * per)
+        x, cos_t, sin_t = gathered(*group)
         raw = dot(x, w[:, q_width:])[:count]
         key = turn(raw[:, :HEAD_WIDTH], cos_t, sin_t)
         value = raw[:, HEAD_WIDTH:].astype(jnp.bfloat16)
         tile = jnp.concatenate([key, value], axis=1)
-        tile = tile.reshape(sizes[k] * per, share, 2 * HEAD_WIDTH)
-        kv_own[blocks_of(k)] = tile
-        kv_all[blocks_of(k), pl.ds(c, 1)] = tile[:, None]
+        tile = tile.reshape(group[1] * per, share, 2 * HEAD_WIDTH)
+        kv_own[span] = tile
+        kv_all[span, pl.ds(c, 1)] = tile[:, None]
         for i in range(1, n_cp):
-            keys_to(i, k).start()
+            keys_to(i, group).start()
+
+    def project_queries(k):
+        count = sizes[k] * unit
+        x, cos_t, sin_t = gathered(firsts[k], sizes[k])
         raw_q = dot(x, w[:, :q_width])[:count]
         for h in range(heads):
             q_all[pl.ds(firsts[k] * unit * heads + h * count, count), :] = turn(
@@ -486,67 +505,73 @@
 
             @pl.when(go_right & (o > z + 1))
             def _():
-                rightward(o, k).start()
+                for u in units_of[k]:
+                    rightward(o, u).start()
 
             @pl.when(go_left & (o < z - 1))
             def _():
-                leftward(o, k).start()
+                for u in units_of[k]:
+                    leftward(o, u).start()
 
             @pl.when(jnp.logical_not(go_right | go_left))
             def _():
                 part[o, lines_of(k)] = product
 
     def adjacent(k):
-        @pl.when(z == 0)
-        def _():
-            rightward(1, k).start()
-
-        @pl.when(z == end)
-        def _():
-            leftward(end - 1, k).start()
-
-    def hop(k, h, dests):
-        lines = lines_of(k)
+        for u in units_of[k]:
+            @pl.when(z == 0)
+            def _():
+                rightward(1, u).start()
+
+            @pl.when(z == end)
+            def _():
+                leftward(end - 1, u).start()
+
+    def hop(u, h, dests):
+        lines = pl.ds(*spans[u])
 
         @pl.when(z == h)
         def _():
             for o in list(range(end, h, -1))[dests]:
-                rightward(o, k).wait_recv()
+                rightward(o, u).wait_recv()
                 total = part[o, lines] + from_left[o, lines].astype(jnp.float32)
                 to_right[o, lines] = total.astype(jnp.bfloat16)
-                rightward(o, k).start()
+                rightward(o, u).start()
 
         @pl.when(z == end - h)
         def _():
             for o in list(range(end - h))[dests]:
-                leftward(o, k).wait_recv()
+                leftward(o, u).wait_recv()
                 total = part[o, lines] + from_right[o, lines].astype(jnp.float32)
                 to_left[o, lines] = total.astype(jnp.bfloat16)
-                leftward(o, k).start()
-
-    def finish(k):
-        lines = lines_of(k)
+                leftward(o, u).start()
+
+    def finish(u):
+        lines = pl.ds(*spans[u])
 
         @pl.when(z > 0)
         def _():
-            rightward(z, k).wait_recv()
+            rightward(z, u).wait_recv()
             part[z, lines] += from_left[z, lines].astype(jnp.float32)
 
         @pl.when(z < end)
         def _():
-            leftward(z, k).wait_recv()
+            leftward(z, u).wait_recv()
             part[z, lines] += from_right[z, lines].astype(jnp.float32)
 
         summed = part[z, lines].astype(jnp.bfloat16)
-        done[blocks_of(k)] = summed.reshape(sizes[k] * per, share, width)
+        taken = pl.ds(spans[u][0] // share, spans[u][1] // share)
+        done[taken] = summed.reshape(spans[u][1] // share, share, width)
 
     def arrive(k):
-        landed_keys = kv_all.at[blocks_of(k), pl.ds(0, n_cp - 1)]
-        pltpu.make_async_copy(landed_keys, landed_keys, k_recv.at[k]).wait()
+        for first, size in groups[k]:
+            keys = kv_all.at[pl.ds(first * per, size * per), pl.ds(0, n_cp - 1)]
+            pltpu.make_async_copy(keys, keys, k_recv.at[first]).wait()
 
     def reduce(k, h, dests=slice(None)):
         with jax.named_scope(f"reduce{k}{h}"):
-            hop(k, h, dests)
+            for u in units_of[k]:
+                hop(u, h, dests)
 
     with jax.named_scope("fill"):
         for source in range(n_cp):
@@ -556,26 +581,21 @@
                 flow(source, 0, False)
             if source < LEAD:
                 flow(source, 0, True)
-        for source in range(LEAD):
+        for source in range(2):
             for d in range(1, end):
                 flow(source, d, False)
-            if source == 0:
+            if source == 1:
                 flow(2, 0, False)
-            if source == LEAD - 1:
-                for d in range(2, end):
-                    flow(0, d, True)
             if end > 1:
                 flow(source, 1, True)
-        for source in range(1, LEAD):
+        for source in range(2):
             for d in range(2, end):
                 flow(source, d, True)
         flow(LEAD, 0, True)
-        flow(LEAD, 0, False)
-        far(LEAD)
-        flow(LEAD + 1, 0, True)
+        far(2)
         ends(0)
     pltpu.make_async_copy(w, w, w_sem).wait()
-    passed, reached = LEAD, LEAD - 1
+    passed, reached = 2, 1
 
     def pass_on(fars, nears):
         nonlocal passed, reached
@@ -587,7 +607,7 @@
             near(reached)
 
     parts = (slice(0, 1), slice(1, None))
-    hops = [(k, h, p) for k in range(last) for h in range(1, end) for p in range(2)]
+    hops = [(k, h, p) for k in range(last) for h in range(1, end) for p in range(min(2, n_tp - 1 - h))]
     held = {}
 
     def run(k, h, *wanted):
@@ -596,12 +616,24 @@
                 hops.remove((k, h, p))
                 reduce(k, h, parts[p])
 
+    def weave(k):
+        left = [(h, p) for e, h, p in hops if e == k]
+        with jax.named_scope("weave"):
+            for u in units_of[k]:
+                for h, p in left:
+                    hop(u, h, parts[p])
+        for h, p in left:
+            hops.remove((k, h, p))
+
     def projection(k):
         pass_on(0, firsts[k + 1] - 1)
-        for source in range(max(firsts[k], 1), firsts[k + 1]):
-            ends(source)
-        with jax.named_scope("project"):
-            project(k)
+        for group in groups[k]:
+            for source in range(max(group[0], 1), group[0] + group[1]):
+                ends(source)
+            with jax.named_scope("keys"):
+                project_keys(group)
+        with jax.named_scope("queries"):
+            project_queries(k)
 
     def attention(k):
         with jax.named_scope("attend"):
@@ -615,17 +647,17 @@
         for k in chosen:
             adjacent(k)
 
-    if last == 5:
+    if last == 4:
         plan = [
             (projection, 0), (pass_on, 5, 3), (attention, 0), (pass_on, 6, 4),
             (result, 0), (adjacents, 0),
             (projection, 1), (pass_on, n_cp, 6), (attention, 1), (pass_on, n_cp, n_cp),
             (result, 1), (adjacents, 1), (run, 0, 1, 0, 1),
-            (projection, 2), (projection, 3), (attention, 2), (run, 1, 1, 0),
-            (result, 2), (run, 1, 1, 1), (run, 0, 2, 0, 1),
-            (projection, 4), (attention, 3), (run, 2, 1, 0), (result, 3), (run, 2, 1, 1),
-            (run, 1, 2, 0, 1), (attention, 4), (run, 3, 1, 0), (result, 4), (adjacents, 2, 3, 4),
-            (run, 3, 1, 1), (run, 2, 2, 0, 1), (run, 4, 1, 0), (run, 3, 2, 0, 1),
+            (projection, 2), (attention, 2), (run, 1, 1, 0),
+            (result, 2), (adjacents, 2), (run, 1, 1, 1), (run, 0, 2, 0),
+            (projection, 3), (run, 1, 2, 0), (run, 2, 1, 0), (attention, 3),
+            (result, 3), (adjacents, 3),
+            (run, 2, 1, 1), (run, 2, 2, 0), (run, 3, 1, 0), (weave, 3),
         ]
     else:
         plan = []
@@ -637,8 +669,8 @@
     for k, h, p in list(hops):
         reduce(k, h, parts[p])
     with jax.named_scope("finish"):
-        for k in range(last):
-            finish(k)
+        for u in range(len(spans)):
+            finish(u)
 
     with jax.named_scope("a2a"):
         for b in range(blocks):
@@ -683,7 +715,7 @@
     smem = pl.BlockSpec(memory_space=pltpu.SMEM)
     slab = (n_tp, rows, width)
     kv_width = 2 * HEAD_WIDTH
-    sums = dma((n_tp - 1, len(sizes)))
+    sums = dma((n_tp - 1, len(sizes) - 1 + sizes[-1] * per))
     flops = 2 * rows * (wq.shape[0] * (wq.shape[1] + kv_width) + wo.shape[0] * wo.shape[1])
     out = pl.pallas_call(
         functools.partial(fused_kernel, n_cp, n_tp, sizes, bounds.shape[0]),
@@ -691,6 +723,7 @@
         in_specs=[smem, hbm, hbm, hbm, hbm, hbm, vmem],
         out_specs=vmem,
         scratch_shapes=[
+            pltpu.VMEM((per, n_cp, share, width), bf),
             pltpu.VMEM((n_tp, blocks, share, width), bf),
             pltpu.VMEM((wq.shape[0], wq.shape[1] + kv_width), bf),
             pltpu.VMEM((n_tp, wo.shape[0], width), bf),
@@ -705,8 +738,8 @@
             pltpu.VMEM((blocks, share, width), bf),
             pltpu.VMEM((per, n_cp, share, width), bf),
             pltpu.SMEM((blocks,), i32),
-            dma, dma, dma, dma, dma((n_cp,)), dma, dma, dma((n_tp, n_cp)),
-            dma, dma((len(sizes),)), dma, dma, sums, sums, dma, dma,
+            dma, dma, dma, dma, dma, dma((n_cp,)), dma, dma, dma((n_tp, n_cp)),
+            dma, dma((n_cp,)), dma, dma, sums, sums, dma, dma,
         ],
         compiler_params=pltpu.CompilerParams(
             collective_id=1, has_side_effects=True, vmem_limit_bytes=VMEM_LIMIT

time: 80.2 us -> 78.4 us (0.978)
  Pallas kernels: 77.9 us -> 76.6 us
    pallas_call x1, Pallas kernels: 77.9 us -> 76.6 us  [fused_call(): pl.pallas_call(functools.partial(fused_kernel, n_cp, n_tp, sizes, bounds....]
where the time goes in v4:
time: 78.4 us; the launch traced here: 78.2 us
  Pallas kernels  76.6 us (98%)
  local copies, waits for them, and re-layouts  0.88 us (1%)
    pallas_call x1, Pallas kernels, fused_call(): pl.pallas_call(functools.partial(fused_kernel, n_cp, n_tp, sizes, bounds....  76.6 us

profile of v4, /device:TPU:1, one launch (start us, length us, event | category | flops | bytes accessed | tf_op | source)
XLA Modules:
  0.0 78.2 jit_solution(17324768460972865758)
XLA Ops:
  0.0 0.7 pad_add_fusion.table
  0.8 0.1 broadcast_in_dim_tile.3.inverse
  0.9 76.6 %shard_map.73 = bf16[2,8,16,1024]{3,2,1,0:T(8,128)(2,1)S(1)} custom-call(s32[25]{0:T(128)S(1)} %pad_add_fusion.table, bf16[2,8,16,1024]{3,2,1,0:T(8,128)(2,1)} %bitcast.3, bf16[4096,1024]{1,0:T(8,128)(2,1)} %wq_hbm.1, bf16[4096,128]{1,0:T(8,128)(2,1)} %wk_hbm.1, bf16[4096,128]{1,0:T(8,128)(2,1)} %wv_hbm.1, bf16[1024,4096]{1,0:T(8,128)(2,1)} %wo_hbm.1, ...), custom_call_target="tpu_custom_call" | custom-call | flops 4831838208 | bytes 20971520 | tf_op jit(solution)/shard_map/pallas_call | solution.py:720
  77.5 0.8 %copy.9 = bf16[256,1024]{1,0:T(8,128)(2,1)} copy(bf16[256,1024]{1,0:T(8,128)(2,1)S(1)} %bitcast.2) | data formatting | bytes 1048576
  (2 shorter events, 0.0 us)

commit v5 on v4

--- a/solution.py
+++ b/solution.py
@@ -258,8 +258,18 @@
     greet(n_cp, n_tp)
     staged.wait()
 
+    def across(i):
+        peer, bit = 0, 1
+        while bit < n_cp:
+            mine_bit = lax.rem(lax.div(c, bit), 2)
+            peer += bit * (1 - mine_bit if i // bit % 2 else mine_bit)
+            bit *= 2
+        return peer
+
+    peers = range(n_cp - 1, 0, -1)
+
     def spread(i):
-        peer = lax.rem(c + i, n_cp)
+        peer = across(i)
         return pltpu.make_async_remote_copy(
             src_ref=mine.at[:, peer], dst_ref=rows.at[z, pl.ds(c * per, per)],
             send_sem=s_send, recv_sem=s_recv.at[i],
@@ -286,7 +296,7 @@
         return pltpu.make_async_remote_copy(
             src_ref=kv_own.at[span], dst_ref=kv_all.at[span, c],
             send_sem=k_send, recv_sem=k_recv.at[group[0]],
-            device_id={"cp": lax.rem(c + i, n_cp)}, device_id_type=MESH,
+            device_id={"cp": across(i)}, device_id_type=MESH,
         )
 
     def rightward(o, u):
@@ -306,14 +316,14 @@
         )
 
     def final(i):
-        peer = lax.rem(c + i, n_cp)
+        peer = across(i)
         return pltpu.make_async_remote_copy(
             src_ref=outgoing.at[pl.ds(peer * per, per)], dst_ref=landed.at[:, c],
             send_sem=a_send, recv_sem=a_recv,
             device_id={"cp": peer}, device_id_type=MESH,
         )
 
-    for i in range(1, n_cp):
+    for i in peers:
         spread(i).start()
     for copy in weights:
         copy.start()
@@ -345,7 +355,8 @@
     def take(source):
         @pl.when(source != c)
         def _():
-            spread(lax.rem(c - source + n_cp, n_cp)).wait_recv()
+            landing = rows.at[z, pl.ds(source * per, per)]
+            pltpu.make_async_copy(landing, landing, s_recv.at[across(source)]).wait()
 
     def end_sends(source):
         @pl.when(z == 0)
@@ -419,7 +430,7 @@
         tile = tile.reshape(group[1] * per, share, 2 * HEAD_WIDTH)
         kv_own[span] = tile
         kv_all[span, pl.ds(c, 1)] = tile[:, None]
-        for i in range(1, n_cp):
+        for i in peers:
             keys_to(i, group).start()
 
     def project_queries(k):
@@ -675,13 +686,13 @@
     with jax.named_scope("a2a"):
         for b in range(blocks):
             outgoing[b] = done[order[b]]
-        for i in range(1, n_cp):
+        for i in peers:
             final(i).start()
         out_ref[:, pl.ds(c, 1)] = outgoing[pl.ds(c * per, per)][:, None]
         others = landed.at[:, pl.ds(0, n_cp - 1)]
         pltpu.make_async_copy(others, others, a_recv).wait()
         for i in range(1, n_cp):
-            source = lax.rem(c - i + n_cp, n_cp)
+            source = across(i)
             out_ref[:, pl.ds(source, 1)] = landed[:, pl.ds(source, 1)]
 
     def drain(ref, sem):

time: 78.4 us -> 77.9 us (level); the launches traced: 78.2 us -> 76.6 us
  Pallas kernels: 76.6 us -> 75 us
    pallas_call x1, Pallas kernels: 76.6 us -> 75 us  [fused_call(): pl.pallas_call(functools.partial(fused_kernel, n_cp, n_tp, sizes, bounds....]
where the time goes in v5:
time: 77.9 us; the launch traced here: 76.6 us
  Pallas kernels  75 us (96%)
  local copies, waits for them, and re-layouts  0.88 us (1%)
    pallas_call x1, Pallas kernels, fused_call(): pl.pallas_call(functools.partial(fused_kernel, n_cp, n_tp, sizes, bounds....  75 us

profile of v5, /device:TPU:1, one launch (start us, length us, event | category | flops | bytes accessed | tf_op | source)
XLA Modules:
  0.0 76.6 jit_solution(6371810626000535510)
XLA Ops:
  0.0 0.7 pad_add_fusion.table
  0.8 0.1 broadcast_in_dim_tile.3.inverse
  0.9 75.0 %shard_map.73 = bf16[2,8,16,1024]{3,2,1,0:T(8,128)(2,1)S(1)} custom-call(s32[25]{0:T(128)S(1)} %pad_add_fusion.table, bf16[2,8,16,1024]{3,2,1,0:T(8,128)(2,1)} %bitcast.3, bf16[4096,1024]{1,0:T(8,128)(2,1)} %wq_hbm.1, bf16[4096,128]{1,0:T(8,128)(2,1)} %wk_hbm.1, bf16[4096,128]{1,0:T(8,128)(2,1)} %wv_hbm.1, bf16[1024,4096]{1,0:T(8,128)(2,1)} %wo_hbm.1, ...), custom_call_target="tpu_custom_call" | custom-call | flops 4831838208 | bytes 20971520 | tf_op jit(solution)/shard_map/pallas_call | solution.py:731
  75.8 0.8 %copy.9 = bf16[256,1024]{1,0:T(8,128)(2,1)} copy(bf16[256,1024]{1,0:T(8,128)(2,1)S(1)} %bitcast.2) | data formatting | bytes 1048576
  (2 shorter events, 0.0 us)
